TPU v7x, 256 devices: a whole 4x4x8 slice. The times are simulated.
256 devices in a mesh: bev: 64 (over z, x, core), scene: 4 (over y).
Axes of the slice: x: 4, y: 4, z: 8, core: 2. Of those that a mesh axis runs over, the one named last changes fastest.
Arguments:
- context: bfloat16 [4, 80, 16384], P('scene', None, 'bev'), may hold values from -24 to 24
- depth_logits: float32 [4, 112, 16384], P('scene', None, 'bev'), may hold values from -20 to 300
- send_count: int32 [4, 64, 64], P('scene', 'bev'), may hold values from 0 to 1024, as said below
- slot_point: int32 [4, 64, 64, 1024], P('scene', 'bev'), may hold values from 0 to 28671, as said below
- slot_cell: int32 [4, 64, 64, 1024], P('scene', 'bev'), may hold values from 0 to 255
Outputs:
- bev_features: bfloat16 [16384, 320], P(('bev', 'scene'))
Inputs may be any that keep to these rules, and one draw needn't show every extreme that they name: `send_count`: one entry is 1024 in every pixel block's row. `slot_point`: the live slots of one pixel block name distinct points; slots at or past the count are unused.
All inputs are finite; a program needn't handle non-finite values.
Results may differ from a plain program's by a relative error of at most 0.0062.
Values may be sent and summed in bfloat16 or wider, within the bound.
No kernel may reach another device: no remote copies, remote signals or barrier semaphores. Data moves between devices by JAX's collectives and lax.ppermute only.
A program may use at most 128 MiB of HBM per device.

v0:
```python
import jax
import jax.numpy as jnp
from jax import lax
from jax.sharding import PartitionSpec as P

GRID = 128


def in_blocks(x, dim, devices):
    before, after = (x.shape[:dim], x.shape[dim + 1 :])
    return jnp.moveaxis(x.reshape(*before, devices, -1, *after), dim, 0)


def sum_at_owner(x, axis, dim):
    devices = lax.axis_size(axis)
    tiles = lax.all_to_all(in_blocks(x, dim, devices), axis, 0, 0, tiled=True)
    return jnp.sum(tiles.astype(jnp.float32), axis=0)


def pool_each(values, cell_ids, strip_cells):
    onehot = (
        cell_ids[:, :, None] == jnp.arange(strip_cells, dtype=jnp.int32)[None, None, :]
    ).astype(jnp.bfloat16)
    return jnp.einsum("gcs,gsn->gnc", values, onehot, preferred_element_type=jnp.float32)


def select_points(point_ids, context_map, depth_prob):
    pix_block = context_map.shape[1]
    depth_bins = depth_prob.shape[0]
    depth_bin = point_ids // pix_block
    pixel_ids = point_ids % pix_block
    pixel_hot = (
        pixel_ids[:, :, None] == jnp.arange(pix_block, dtype=jnp.int32)[None, None, :]
    ).astype(jnp.bfloat16)
    depth_hot = (
        depth_bin[:, :, None] == jnp.arange(depth_bins, dtype=jnp.int32)[None, None, :]
    ).astype(jnp.bfloat16)
    features = jnp.einsum("nsp,cp->ncs", pixel_hot, context_map, preferred_element_type=jnp.float32)
    prob_rows = jnp.einsum("nsk,kp->nsp", depth_hot, depth_prob, preferred_element_type=jnp.float32)
    weight = jnp.sum(prob_rows * pixel_hot.astype(jnp.float32), axis=2)
    return (features * weight[:, None, :]).astype(jnp.bfloat16)


def body(context, depth_logits, send_count, slot_point, slot_cell):
    strips = lax.axis_size("bev")
    scenes = lax.axis_size("scene")
    strip_cells = GRID * GRID // strips
    channels = context.shape[1]
    capacity = slot_point.shape[3]
    depth_prob = jax.nn.softmax(depth_logits[0], axis=0).astype(jnp.bfloat16)
    context_map = context[0]
    counts = send_count[0, 0]
    points = slot_point[0, 0]
    live_mask = jnp.arange(capacity, dtype=jnp.int32)[None, :] < counts[:, None]
    targets = jnp.where(live_mask, slot_cell[0, 0], strip_cells)
    values = select_points(points, context_map, depth_prob)
    strip_sum = sum_at_owner(
        pool_each(values, targets, strip_cells)
        .reshape(strip_cells * lax.axis_size("bev"), channels)
        .astype(jnp.bfloat16),
        "bev",
        0,
    )
    quarter = strip_cells // scenes
    rounded = strip_sum.astype(jnp.bfloat16).reshape(scenes, quarter, 1, channels)
    moved = lax.all_to_all(rounded, "scene", split_axis=0, concat_axis=2, tiled=True)
    return moved.reshape(quarter, scenes * channels)


def solution(mesh):
    return jax.shard_map(
        body,
        mesh=mesh,
        in_specs=(
            P("scene", None, "bev"),
            P("scene", None, "bev"),
            P("scene", "bev", None),
            P("scene", "bev", None, None),
            P("scene", "bev", None, None),
        ),
        out_specs=P(("bev", "scene"), None),
        check_vma=False,
    )
```

profile of v0, /device:TPU:1, one launch (start us, length us, event | category | flops | bytes accessed | tf_op | source)
XLA Modules:
  0.0 141.4 jit_solution(11307070710234492354)
XLA Ops:
  0.0 0.0 copy-start
  0.0 0.9 reduce_max.9
  0.9 0.9 fusion.13
  1.9 1.3 add_select_fusion
  3.2 19.7 %multiply_reduce_fusion = f32[64,1024]{1,0:T(8,128)S(1)} fusion(s32[64,1024]{1,0:T(8,128)S(1)} %get-tuple-element.6, s32[64,1024]{1,0:T(8,128)S(1)} %get-tuple-element.5, f32[1,112,256]{2,1,0:T(8,128)} %param.6, f32[256]{0:T(256)S(1)} %fusion.13, f32[256]{0:T(256)S(1)} %reduce_max.9), kind=kOutput, calls=%fused_computation | convolution fusion | flops 3849342976 | bytes 903168 | tf_op jit(solution)/shard_map/nsk,kp->nsp/dot_general | solution.py:39
  22.9 0.0 copy-done
  22.9 15.2 %multiply_convert_fusion.7 = bf16[64,1024,80]{1,2,0:T(8,128)(2,1)S(1)} fusion(f32[64,1024]{1,0:T(8,128)S(1)} %multiply_reduce_fusion, s32[64,1024]{1,0:T(8,128)S(1)} %get-tuple-element.6, bf16[1,80,256]{2,1,0:T(8,128)(2,1)S(1)} %copy-done), kind=kOutput, calls=%fused_computation.10.clone.clone.clone.clone.2 | convolution fusion | flops 2711617536 | bytes 11051008 | tf_op jit(solution)/shard_map/nsp,cp->ncs/dot_general | solution.py:38
  38.1 18.1 %fusion.8 = bf16[64,256,80]{1,2,0:T(8,128)(2,1)S(1)} fusion(s32[64,1024]{1,0:T(8,128)S(1)} %get-tuple-element.7, bf16[64,1024,80]{1,2,0:T(8,128)(2,1)S(1)} %multiply_convert_fusion.7), kind=kOutput, calls=%fused_computation.13 | convolution fusion | flops 2702442496 | bytes 13369344 | tf_op jit(solution)/shard_map/gcs,gsn->gnc/dot_general | solution.py:24
  56.1 75.5 %all_to_all.20 = bf16[64,256,80]{1,2,0:T(8,128)(2,1)S(1)} all-to-all(bf16[64,256,80]{1,2,0:T(8,128)(2,1)S(1)} %fusion.8), channel_id=1, replica_groups=mesh['bev'=64,'scene'=4] {'bev'}, dimensions={0} | all-to-all | bytes 5242880 | tf_op jit(solution)/shard_map/all_to_all | solution.py:16
  131.6 0.4 reduce_sum.32
  132.0 0.1 copy.9
  132.1 8.5 %all_to_all.21 = bf16[4,64,1,80]{3,1,2,0:T(8,128)(2,1)S(1)} all-to-all(bf16[4,64,1,80]{3,1,2,0:T(8,128)(2,1)S(1)} %bitcast.62), channel_id=1, replica_groups=mesh['bev'=64,'scene'=4] {'scene'}, dimensions={0} | all-to-all | bytes 81920 | tf_op jit(solution)/shard_map/all_to_all | solution.py:66
  140.6 0.1 copy.11
  140.7 0.7 reshape.91
Async XLA Ops:
  0.0 22.9 %copy-start = (bf16[1,80,256]{2,1,0:T(8,128)(2,1)S(1)}, bf16[1,80,256]{2,1,0:T(8,128)(2,1)}, u32[]{:S(2)}) copy-start(bf16[1,80,256]{2,1,0:T(8,128)(2,1)} %param.5) | copy-start | bytes 122884
where the time goes:
time: 142 us; the launch traced here: 141 us
  blocking collectives  84 us (59%)
  matrix products  53 us (37%)
  other arithmetic  3.52 us (2%)
    all_to_all x1, blocking collectives, sum_at_owner(): tiles = lax.all_to_all(in_blocks(x, dim, devices), axis, 0, 0, tiled=True)  75.5 us
    dot_general x1, matrix products, select_points(): jnp.einsum('nsk,kp->nsp', depth_hot, depth_prob, preferred_element_type=j...  19.7 us
    dot_general x1, matrix products, pool_each(): jnp.einsum('gcs,gsn->gnc', values, onehot, preferred_element_type=jnp.flo...  18.1 us
    dot_general x1, matrix products, select_points(): jnp.einsum('nsp,cp->ncs', pixel_hot, context_map, preferred_element_type=...  15.2 us
    all_to_all x1, blocking collectives, body(): lax.all_to_all(rounded, 'scene', split_axis=0, concat_axis=2, tiled=True)  8.45 us

commit v1 on v0

v1 whole, which is shorter than its diff:
```python
import jax
import jax.numpy as jnp
from jax import lax
from jax.experimental import pallas as pl
from jax.experimental.pallas import tpu as pltpu
from jax.sharding import Mesh, PartitionSpec as P

C = 80
DEPTH = 112
PIX = 256
CELLS = 256
STRIPS = 64
CAP = 1024
CHUNK = 256
NCH = CAP // CHUNK
TILES = CAP // 128
GROUP = 8
ZS = 8
SLOT_ROWS = 3 * ZS * NCH
ROWS = SLOT_ROWS + C
BATCH_A = 8
BATCH_B = 4

BF = jnp.bfloat16
F32 = jnp.float32


def iota16(lanes):
    return lax.broadcasted_iota(jnp.int32, (16, lanes), 0).astype(F32).astype(BF)


def onehot_rows(row, count):
    lanes = row.shape[1]
    base = jnp.broadcast_to(row, (16, lanes)).astype(BF) - iota16(lanes)
    one, zero = jnp.ones((16, lanes), BF), jnp.zeros((16, lanes), BF)
    return jnp.concatenate(
        [jnp.where(base == jnp.asarray(16.0 * g, BF), one, zero) for g in range(count // 16)], axis=0
    )


def send_kernel(count_ref, logits_ref, ctx_ref, point_ref, cell_ref, out_ref, prob_ref, weight_ref, pixel_ref, target_ref):
    logits = logits_ref[...]
    shifted = jnp.exp(logits - jnp.max(logits, axis=0, keepdims=True))
    prob_ref[...] = (shifted / jnp.sum(shifted, axis=0, keepdims=True)).astype(BF)
    weight_ref[...] = jnp.zeros(weight_ref.shape, F32)

    def chunks_of(strip):
        inside = jnp.minimum(strip, STRIPS - 1)
        return jnp.maximum((count_ref[inside] + (CHUNK - 1)) // CHUNK, 1)

    total = lax.fori_loop(0, STRIPS, lambda d, s: s + chunks_of(d), jnp.int32(0))
    bins = lax.broadcasted_iota(jnp.int32, (DEPTH, CHUNK), 0)

    def step(_, carry):
        strip, j = carry
        for _ in range(BATCH_A):
            row = jnp.minimum(strip, STRIPS - 1)
            lane = pl.multiple_of(j * CHUNK, CHUNK)
            point = point_ref[pl.ds(row, 1), pl.ds(lane, CHUNK)]
            pixel = (point & (PIX - 1)).astype(F32)
            hot = onehot_rows(pixel, PIX)
            column = jnp.dot(prob_ref[...], hot, preferred_element_type=F32)
            bin_id = jnp.broadcast_to(point >> 8, (DEPTH, CHUNK))
            weight = jnp.sum(jnp.where(bin_id == bins, column, 0.0), axis=0, keepdims=True)
            weight_ref[2 * j, pl.ds(row, 1), :] = weight[:, :128]
            weight_ref[2 * j + 1, pl.ds(row, 1), :] = weight[:, 128:]
            last = j + 1 >= chunks_of(strip)
            strip = jnp.where(last, strip + 1, strip)
            j = jnp.where(last, 0, j + 1)
        return strip, j

    lax.fori_loop(0, (total + BATCH_A - 1) // BATCH_A, step, (jnp.int32(0), jnp.int32(0)))

    sub = lax.broadcasted_iota(jnp.int32, (GROUP, CAP), 0)
    slot = lax.broadcasted_iota(jnp.int32, (GROUP, CAP), 1)
    for z in range(ZS):
        rows = slice(z * GROUP, (z + 1) * GROUP)
        limit = jnp.zeros((GROUP, CAP), jnp.int32)
        for dest in range(GROUP):
            limit = jnp.where(sub == dest, count_ref[z * GROUP + dest], limit)
        pixel = jnp.where(slot < limit, point_ref[rows, :] & (PIX - 1), -1).astype(F32)
        cell = cell_ref[rows, :].astype(F32)
        for t in range(TILES):
            pixel_ref[t, rows, :] = pixel[:, t * 128 : (t + 1) * 128]
            target_ref[t, rows, :] = cell[:, t * 128 : (t + 1) * 128]
    context = ctx_ref[...]
    for dest in range(GROUP):
        for kind, ref in enumerate((weight_ref, pixel_ref, target_ref)):
            for half in range(2):
                stacked = jnp.concatenate(
                    [ref[2 * i + half, pl.ds(dest, ZS, stride=GROUP), :] for i in range(NCH)], axis=0
                )
                out_ref[
                    dest, kind * ZS * NCH : (kind + 1) * ZS * NCH, half * 128 : (half + 1) * 128
                ] = stacked.astype(BF)
        out_ref[dest, SLOT_ROWS:ROWS, :] = context


def pool_kernel(in_ref, out_ref, slots_ref, acc_ref, val_ref, word_ref):
    for src in range(GROUP):
        slots_ref[src * SLOT_ROWS : (src + 1) * SLOT_ROWS, :] = in_ref[src, :SLOT_ROWS, :].astype(F32)
    acc_ref[...] = jnp.zeros(acc_ref.shape, F32)
    val_ref[...] = jnp.zeros(val_ref.shape, BF)

    rows = ZS * NCH
    lane0 = lax.broadcasted_iota(jnp.int32, (ZS, 128), 1) == 0
    digit = jnp.left_shift(1, 3 * lax.broadcasted_iota(jnp.int32, (ZS, 128), 0)).astype(F32)
    total = jnp.int32(0)
    for src in range(GROUP):
        live = jnp.zeros((ZS, 128), F32)
        for j in range(NCH):
            first = slots_ref[src * SLOT_ROWS + rows + j * ZS : src * SLOT_ROWS + rows + (j + 1) * ZS, :128]
            on = first >= 0.0
            if j == 0:
                on = on | True
            live = live + jnp.where(lane0 & on, 1.0, 0.0)
        word_ref[src] = jnp.sum(live * digit).astype(jnp.int32)
        total = total + jnp.sum(live).astype(jnp.int32)
    word_ref[GROUP] = 0

    def step(it, carry):
        src, z, j = carry[:3]
        older = carry[3:]
        now, before = lax.rem(it, 2), lax.rem(it + 1, 2)
        fresh = []
        for b in range(BATCH_B):
            old_row, old_acc = older[2 * b], older[2 * b + 1]
            cell = slots_ref[pl.ds(old_row, 1), :]
            hot = onehot_rows(cell, CELLS)
            part = lax.dot_general(
                val_ref[before, b], hot, (((1,), (1,)), ((), ())), preferred_element_type=F32
            )
            acc_ref[old_acc] = acc_ref[old_acc] + part

            valid = src < GROUP
            source = jnp.where(valid, src, 0)
            row = source * SLOT_ROWS + j * ZS + z
            weight = slots_ref[pl.ds(row, 1), :]
            pixel = slots_ref[pl.ds(row + rows, 1), :]
            hot = onehot_rows(pixel, PIX)
            feature = jnp.dot(in_ref[source, SLOT_ROWS:ROWS, :], hot, preferred_element_type=F32)
            val_ref[now, b] = (feature * weight).astype(BF)
            fresh += [row + 2 * rows, jnp.where(valid, z, ZS)]

            chunks = jnp.right_shift(word_ref[jnp.minimum(src, GROUP)], 3 * z) & 7
            last = j + 1 >= chunks
            j = jnp.where(last, 0, j + 1)
            z = jnp.where(last, z + 1, z)
            wrap = z >= ZS
            z = jnp.where(wrap, 0, z)
            src = jnp.where(wrap, src + 1, src)
        return (src, z, j, *fresh)

    zero = jnp.int32(0)
    start = (zero, zero, zero) + (zero, jnp.int32(ZS)) * BATCH_B
    lax.fori_loop(0, (total + BATCH_B - 1) // BATCH_B + 1, step, start)

    left = lax.broadcasted_iota(jnp.int32, (C // 2, 128), 1) < 64
    for z in range(ZS):
        for t in range(2):
            a = acc_ref[z, : C // 2, t * 128 : (t + 1) * 128]
            b = acc_ref[z, C // 2 :, t * 128 : (t + 1) * 128]
            out_ref[z * 4 + 2 * t] = jnp.where(left, a, pltpu.roll(b, 64, 1)).astype(BF)
            out_ref[z * 4 + 2 * t + 1] = jnp.where(left, pltpu.roll(a, 64, 1), b).astype(BF)


def merge_kernel(in_ref, out_ref):
    parts = []
    for s in range(4):
        total = jnp.zeros((C // 2, 128), F32)
        for z in range(ZS):
            total = total + in_ref[z * 4 + s].astype(F32)
        parts += [total, pltpu.roll(total, 64, 1)]
    stacked = jnp.concatenate(parts, axis=0)
    out_ref[...] = stacked.T[:64, :].astype(BF)


VMEM = pl.BlockSpec(memory_space=pltpu.VMEM)
SMEM = pl.BlockSpec(memory_space=pltpu.SMEM)


def send(counts, logits, context, points, cells):
    return pl.pallas_call(
        send_kernel,
        out_shape=jax.ShapeDtypeStruct((GROUP, ROWS, PIX), BF),
        in_specs=[SMEM, VMEM, VMEM, VMEM, VMEM],
        out_specs=VMEM,
        scratch_shapes=[pltpu.VMEM((DEPTH, PIX), BF)] + [pltpu.VMEM((TILES, STRIPS, 128), F32)] * 3,
        name="send_slots",
    )(counts, logits, context, points, cells)


def pool(slots):
    return pl.pallas_call(
        pool_kernel,
        out_shape=jax.ShapeDtypeStruct((ZS * 4, C // 2, 128), BF),
        in_specs=[VMEM],
        out_specs=VMEM,
        scratch_shapes=[
            pltpu.VMEM((GROUP * SLOT_ROWS, CHUNK), F32),
            pltpu.VMEM((ZS + 1, C, CELLS), F32),
            pltpu.VMEM((2, BATCH_B, C, CHUNK), BF),
            pltpu.SMEM((GROUP + 1,), jnp.int32),
        ],
        name="pool_slots",
    )(slots)


def merge(partials):
    return pl.pallas_call(
        merge_kernel,
        out_shape=jax.ShapeDtypeStruct((64, 4 * C), BF),
        in_specs=[VMEM],
        out_specs=VMEM,
        name="merge_parts",
    )(partials)


def body(context, depth_logits, send_count, slot_point, slot_cell):
    slots = send(send_count[0, 0], depth_logits[0], context[0], slot_point[0, 0], slot_cell[0, 0])
    slots = lax.all_to_all(slots, ("x", "core"), 0, 0, tiled=True)
    partials = pool(slots)
    partials = lax.all_to_all(partials, ("z", "scene"), 0, 0, tiled=True)
    return merge(partials)


def solution(mesh):
    split = Mesh(mesh.devices.reshape(8, 4, 2, 4), ("z", "x", "core", "scene"))
    bev = ("z", "x", "core")
    return jax.shard_map(
        body,
        mesh=split,
        in_specs=(
            P("scene", None, bev),
            P("scene", None, bev),
            P("scene", bev, None),
            P("scene", bev, None, None),
            P("scene", bev, None, None),
        ),
        out_specs=P(("z", "x", "core", "scene"), None),
        check_vma=False,
    )
```

time: 142 us -> 64.9 us (0.46)
  matrix products: 53 us -> 0 us
  blocking collectives: 84 us -> 41.2 us
  Pallas kernels: 0 us -> 23.1 us
  other arithmetic: 3.52 us -> 0 us
    dot_general x3 -> x0, matrix products: 53 us -> none  [the longest x1 19.7 us: select_points(): jnp.einsum('nsk,kp->nsp', depth_hot, depth_prob, preferred_element_type=j...]
    all_to_all x2, blocking collectives: 84 us -> 41.2 us  [the longest x1 22.3 us: body(): partials = lax.all_to_all(partials, ('z', 'scene'), 0, 0, tiled=True)]
    pallas_call x0 -> x3, Pallas kernels: none -> 23.1 us  [the longest x1 13.3 us: pool(): pl.pallas_call(pool_kernel, out_shape=jax.ShapeDtypeStruct((ZS * 4, C //...]
where the time goes in v1:
time: 64.9 us; the launch traced here: 64.3 us
  blocking collectives  41.2 us (63%)
  Pallas kernels  23.1 us (36%)
    all_to_all x1, blocking collectives, body(): partials = lax.all_to_all(partials, ('z', 'scene'), 0, 0, tiled=True)  22.3 us
    all_to_all x1, blocking collectives, body(): slots = lax.all_to_all(slots, ('x', 'core'), 0, 0, tiled=True)  18.9 us
    pallas_call x1, Pallas kernels, pool(): pl.pallas_call(pool_kernel, out_shape=jax.ShapeDtypeStruct((ZS * 4, C //...  13.3 us
    pallas_call x1, Pallas kernels, send(): pl.pallas_call(send_kernel, out_shape=jax.ShapeDtypeStruct((GROUP, ROWS,...  8.03 us
    pallas_call x1, Pallas kernels, merge(): pl.pallas_call(merge_kernel, out_shape=jax.ShapeDtypeStruct((64, 4 * C),...  1.78 us

profile of v1, /device:TPU:1, one launch (start us, length us, event | category | flops | bytes accessed | tf_op | source)
XLA Modules:
  0.0 64.3 jit_solution(18009165497099425)
XLA Ops:
  0.0 8.0 %send_slots.1 = bf16[8,176,256]{2,1,0:T(8,128)(2,1)} custom-call(s32[64]{0:T(128)} %bitcast.9, f32[112,256]{1,0:T(8,128)} %bitcast.7, bf16[80,256]{1,0:T(8,128)(2,1)} %bitcast.8, s32[64,1024]{1,0:T(8,128)} %bitcast.5, s32[64,1024]{1,0:T(8,128)} %bitcast.6), custom_call_target="tpu_custom_call" | custom-call | tf_op jit(solution)/shard_map/send_slots/pallas_call | solution.py:183
  8.0 18.9 %all_to_all.10.in_ref = bf16[8,176,256]{2,1,0:T(8,128)(2,1)} all-to-all(bf16[8,176,256]{2,1,0:T(8,128)(2,1)} %send_slots.1), channel_id=1, replica_groups=mesh['z'=8,'x'=4,'core'=2,'scene'=4] {'x','core'}, dimensions={0} | all-to-all | bytes 1441792 | tf_op jit(solution)/shard_map/all_to_all | solution.py:221
  26.9 13.3 %pool_slots.1 = bf16[32,40,128]{2,1,0:T(8,128)(2,1)} custom-call(bf16[8,176,256]{2,1,0:T(8,128)(2,1)} %all_to_all.10.in_ref), custom_call_target="tpu_custom_call" | custom-call | tf_op jit(solution)/shard_map/pool_slots/pallas_call | solution.py:194
  40.2 22.3 %all_to_all.11.in_ref = bf16[32,40,128]{2,1,0:T(8,128)(2,1)} all-to-all(bf16[32,40,128]{2,1,0:T(8,128)(2,1)} %pool_slots.1), channel_id=1, replica_groups=mesh['z'=8,'x'=4,'core'=2,'scene'=4] {'z','scene'}, dimensions={0} | all-to-all | bytes 655360 | tf_op jit(solution)/shard_map/all_to_all | solution.py:223
  62.5 1.8 %merge_parts.1 = bf16[64,320]{1,0:T(8,128)(2,1)} custom-call(bf16[32,40,128]{2,1,0:T(8,128)(2,1)} %all_to_all.11.in_ref), custom_call_target="tpu_custom_call" | custom-call | tf_op jit(solution)/shard_map/merge_parts/pallas_call | solution.py:210

commit v2 on v1

--- a/solution.py
+++ b/solution.py
@@ -13,13 +13,12 @@
 CAP = 1024
 CHUNK = 256
 NCH = CAP // CHUNK
-TILES = CAP // 128
 GROUP = 8
 ZS = 8
 SLOT_ROWS = 3 * ZS * NCH
 ROWS = SLOT_ROWS + C
-BATCH_A = 8
-BATCH_B = 4
+BATCH_A = 16
+BATCH_B = 8
 
 BF = jnp.bfloat16
 F32 = jnp.float32
@@ -35,21 +34,37 @@
     one, zero = jnp.ones((16, lanes), BF), jnp.zeros((16, lanes), BF)
     return jnp.concatenate(
         [jnp.where(base == jnp.asarray(16.0 * g, BF), one, zero) for g in range(count // 16)], axis=0
-    )
-
-
-def send_kernel(count_ref, logits_ref, ctx_ref, point_ref, cell_ref, out_ref, prob_ref, weight_ref, pixel_ref, target_ref):
+    ).astype(jnp.float8_e4m3fn)
+
+
+def send_kernel(
+    count_ref, logits_hbm, ctx_hbm, point_hbm, cell_hbm, out_ref,
+    logits_ref, ctx_ref, point_ref, cell_ref, prob_ref, weight_ref, pixel_ref, target_ref, sems,
+):
+    pairs = ((logits_hbm, logits_ref), (point_hbm, point_ref), (cell_hbm, cell_ref), (ctx_hbm, ctx_ref))
+    copies = [pltpu.make_async_copy(src, dst, sems.at[i]) for i, (src, dst) in enumerate(pairs)]
+    for copy in copies:
+        copy.start()
+    weight_ref[...] = jnp.zeros(weight_ref.shape, F32)
+    pixel_ref[...] = jnp.full(pixel_ref.shape, -1.0, F32)
+    target_ref[...] = jnp.zeros(target_ref.shape, F32)
+
+    def chunks_of(strip):
+        inside = jnp.minimum(strip, STRIPS - 1)
+        return (count_ref[inside] + (CHUNK - 1)) // CHUNK
+
+    total = jnp.int32(0)
+    for d in range(STRIPS):
+        total = total + jnp.maximum((count_ref[d] + (CHUNK - 1)) // CHUNK, 1)
+
+    copies[0].wait()
     logits = logits_ref[...]
     shifted = jnp.exp(logits - jnp.max(logits, axis=0, keepdims=True))
     prob_ref[...] = (shifted / jnp.sum(shifted, axis=0, keepdims=True)).astype(BF)
-    weight_ref[...] = jnp.zeros(weight_ref.shape, F32)
-
-    def chunks_of(strip):
-        inside = jnp.minimum(strip, STRIPS - 1)
-        return jnp.maximum((count_ref[inside] + (CHUNK - 1)) // CHUNK, 1)
-
-    total = lax.fori_loop(0, STRIPS, lambda d, s: s + chunks_of(d), jnp.int32(0))
     bins = lax.broadcasted_iota(jnp.int32, (DEPTH, CHUNK), 0)
+    slot = lax.broadcasted_iota(jnp.int32, (1, CHUNK), 1)
+    copies[1].wait()
+    copies[2].wait()
 
     def step(_, carry):
         strip, j = carry
@@ -62,8 +77,11 @@
             column = jnp.dot(prob_ref[...], hot, preferred_element_type=F32)
             bin_id = jnp.broadcast_to(point >> 8, (DEPTH, CHUNK))
             weight = jnp.sum(jnp.where(bin_id == bins, column, 0.0), axis=0, keepdims=True)
-            weight_ref[2 * j, pl.ds(row, 1), :] = weight[:, :128]
-            weight_ref[2 * j + 1, pl.ds(row, 1), :] = weight[:, 128:]
+            pixel = jnp.where(slot + lane < count_ref[row], pixel, -1.0)
+            cell = cell_ref[pl.ds(row, 1), pl.ds(lane, CHUNK)].astype(F32)
+            place = (row & (GROUP - 1)) * ZS + (row >> 3)
+            for ref, value in ((weight_ref, weight), (pixel_ref, pixel), (target_ref, cell)):
+                ref[j, pl.ds(place, 1), :] = value
             last = j + 1 >= chunks_of(strip)
             strip = jnp.where(last, strip + 1, strip)
             j = jnp.where(last, 0, j + 1)
@@ -71,28 +89,12 @@
 
     lax.fori_loop(0, (total + BATCH_A - 1) // BATCH_A, step, (jnp.int32(0), jnp.int32(0)))
 
-    sub = lax.broadcasted_iota(jnp.int32, (GROUP, CAP), 0)
-    slot = lax.broadcasted_iota(jnp.int32, (GROUP, CAP), 1)
-    for z in range(ZS):
-        rows = slice(z * GROUP, (z + 1) * GROUP)
-        limit = jnp.zeros((GROUP, CAP), jnp.int32)
-        for dest in range(GROUP):
-            limit = jnp.where(sub == dest, count_ref[z * GROUP + dest], limit)
-        pixel = jnp.where(slot < limit, point_ref[rows, :] & (PIX - 1), -1).astype(F32)
-        cell = cell_ref[rows, :].astype(F32)
-        for t in range(TILES):
-            pixel_ref[t, rows, :] = pixel[:, t * 128 : (t + 1) * 128]
-            target_ref[t, rows, :] = cell[:, t * 128 : (t + 1) * 128]
+    copies[3].wait()
     context = ctx_ref[...]
     for dest in range(GROUP):
         for kind, ref in enumerate((weight_ref, pixel_ref, target_ref)):
-            for half in range(2):
-                stacked = jnp.concatenate(
-                    [ref[2 * i + half, pl.ds(dest, ZS, stride=GROUP), :] for i in range(NCH)], axis=0
-                )
-                out_ref[
-                    dest, kind * ZS * NCH : (kind + 1) * ZS * NCH, half * 128 : (half + 1) * 128
-                ] = stacked.astype(BF)
+            stacked = jnp.concatenate([ref[i, dest * ZS : (dest + 1) * ZS, :] for i in range(NCH)], axis=0)
+            out_ref[dest, kind * ZS * NCH : (kind + 1) * ZS * NCH, :] = stacked.astype(BF)
         out_ref[dest, SLOT_ROWS:ROWS, :] = context
 
 
@@ -175,17 +177,30 @@
     out_ref[...] = stacked.T[:64, :].astype(BF)
 
 
+PARAMS = pltpu.CompilerParams(vmem_limit_bytes=12 * 1024 * 1024)
 VMEM = pl.BlockSpec(memory_space=pltpu.VMEM)
+HBM = pl.BlockSpec(memory_space=pltpu.HBM)
 SMEM = pl.BlockSpec(memory_space=pltpu.SMEM)
 
 
 def send(counts, logits, context, points, cells):
     return pl.pallas_call(
         send_kernel,
-        out_shape=jax.ShapeDtypeStruct((GROUP, ROWS, PIX), BF),
-        in_specs=[SMEM, VMEM, VMEM, VMEM, VMEM],
+        out_shape=pltpu.VMEM((GROUP, ROWS, PIX), BF),
+        in_specs=[SMEM, HBM, HBM, HBM, HBM],
         out_specs=VMEM,
-        scratch_shapes=[pltpu.VMEM((DEPTH, PIX), BF)] + [pltpu.VMEM((TILES, STRIPS, 128), F32)] * 3,
+        scratch_shapes=[
+            pltpu.VMEM((DEPTH, PIX), F32),
+            pltpu.VMEM((C, PIX), BF),
+            pltpu.VMEM((STRIPS, CAP), jnp.int32),
+            pltpu.VMEM((STRIPS, CAP), jnp.int32),
+            pltpu.VMEM((DEPTH, PIX), BF),
+            pltpu.VMEM((NCH, STRIPS, CHUNK), F32),
+            pltpu.VMEM((NCH, STRIPS, CHUNK), F32),
+            pltpu.VMEM((NCH, STRIPS, CHUNK), F32),
+            pltpu.SemaphoreType.DMA((4,)),
+        ],
+        compiler_params=pltpu.CompilerParams(vmem_limit_bytes=67043328 - 800 * 1024),
         name="send_slots",
     )(counts, logits, context, points, cells)
 
@@ -202,6 +217,7 @@
             pltpu.VMEM((2, BATCH_B, C, CHUNK), BF),
             pltpu.SMEM((GROUP + 1,), jnp.int32),
         ],
+        compiler_params=PARAMS,
         name="pool_slots",
     )(slots)
 
@@ -212,6 +228,7 @@
         out_shape=jax.ShapeDtypeStruct((64, 4 * C), BF),
         in_specs=[VMEM],
         out_specs=VMEM,
+        compiler_params=PARAMS,
         name="merge_parts",
     )(partials)
 

time: 64.9 us -> 54.8 us (0.84)
  Pallas kernels: 23.1 us -> 13.8 us
    pallas_call x1, Pallas kernels: 13.3 us -> 7.02 us  [pool(): pl.pallas_call(pool_kernel, out_shape=jax.ShapeDtypeStruct((ZS * 4, C //...]
    pallas_call x1, Pallas kernels: 8.03 us -> 5.93 us  [send(): pl.pallas_call(send_kernel, out_shape=pltpu.VMEM((GROUP, ROWS, PIX), BF),...]
    all_to_all x1, blocking collectives: 18.9 us -> 17.1 us  [body(): slots = lax.all_to_all(slots, ('x', 'core'), 0, 0, tiled=True)]
    all_to_all x1, blocking collectives: 22.3 us -> 23.5 us  [body(): partials = lax.all_to_all(partials, ('z', 'scene'), 0, 0, tiled=True)]
    pallas_call x1, Pallas kernels: 1.78 us -> 0.8 us  [merge(): pl.pallas_call(merge_kernel, out_shape=jax.ShapeDtypeStruct((64, 4 * C),...]
where the time goes in v2:
time: 54.8 us; the launch traced here: 54.4 us
  blocking collectives  40.6 us (74%)
  Pallas kernels  13.8 us (25%)
    all_to_all x1, blocking collectives, body(): partials = lax.all_to_all(partials, ('z', 'scene'), 0, 0, tiled=True)  23.5 us
    all_to_all x1, blocking collectives, body(): slots = lax.all_to_all(slots, ('x', 'core'), 0, 0, tiled=True)  17.1 us
    pallas_call x1, Pallas kernels, pool(): pl.pallas_call(pool_kernel, out_shape=jax.ShapeDtypeStruct((ZS * 4, C //...  7.02 us
    pallas_call x1, Pallas kernels, send(): pl.pallas_call(send_kernel, out_shape=pltpu.VMEM((GROUP, ROWS, PIX), BF),...  5.93 us

profile of v2, /device:TPU:1, one launch (start us, length us, event | category | flops | bytes accessed | tf_op | source)
XLA Modules:
  0.0 54.4 jit_solution(18020382325652607374)
XLA Ops:
  0.0 5.9 %send_slots.1 = bf16[8,176,256]{2,1,0:T(8,128)(2,1)S(1)} custom-call(s32[64]{0:T(128)} %bitcast.9, f32[112,256]{1,0:T(8,128)} %bitcast.7, bf16[80,256]{1,0:T(8,128)(2,1)} %bitcast.8, s32[64,1024]{1,0:T(8,128)} %bitcast.5, s32[64,1024]{1,0:T(8,128)} %bitcast.6), custom_call_target="tpu_custom_call" | custom-call | tf_op jit(solution)/shard_map/send_slots/pallas_call | solution.py:187
  5.9 17.1 %all_to_all.10.in_ref = bf16[8,176,256]{2,1,0:T(8,128)(2,1)S(1)} all-to-all(bf16[8,176,256]{2,1,0:T(8,128)(2,1)S(1)} %send_slots.1), channel_id=1, replica_groups=mesh['z'=8,'x'=4,'core'=2,'scene'=4] {'x','core'}, dimensions={0} | all-to-all | bytes 1441792 | tf_op jit(solution)/shard_map/all_to_all | solution.py:238
  23.1 7.0 %pool_slots.1 = bf16[32,40,128]{2,1,0:T(8,128)(2,1)S(1)} custom-call(bf16[8,176,256]{2,1,0:T(8,128)(2,1)S(1)} %all_to_all.10.in_ref), custom_call_target="tpu_custom_call" | custom-call | tf_op jit(solution)/shard_map/pool_slots/pallas_call | solution.py:209
  30.1 23.5 %all_to_all.11.in_ref = bf16[32,40,128]{2,1,0:T(8,128)(2,1)S(1)} all-to-all(bf16[32,40,128]{2,1,0:T(8,128)(2,1)S(1)} %pool_slots.1), channel_id=1, replica_groups=mesh['z'=8,'x'=4,'core'=2,'scene'=4] {'z','scene'}, dimensions={0} | all-to-all | bytes 655360 | tf_op jit(solution)/shard_map/all_to_all | solution.py:240
  53.6 0.8 %merge_parts.1 = bf16[64,320]{1,0:T(8,128)(2,1)} custom-call(bf16[32,40,128]{2,1,0:T(8,128)(2,1)S(1)} %all_to_all.11.in_ref), custom_call_target="tpu_custom_call" | custom-call | tf_op jit(solution)/shard_map/merge_parts/pallas_call | solution.py:226

commit v3 on v2

--- a/solution.py
+++ b/solution.py
@@ -17,8 +17,8 @@
 ZS = 8
 SLOT_ROWS = 3 * ZS * NCH
 ROWS = SLOT_ROWS + C
-BATCH_A = 16
-BATCH_B = 8
+BATCH_A = 56
+BATCH_B = 28
 
 BF = jnp.bfloat16
 F32 = jnp.float32
@@ -51,17 +51,17 @@
 
     def chunks_of(strip):
         inside = jnp.minimum(strip, STRIPS - 1)
-        return (count_ref[inside] + (CHUNK - 1)) // CHUNK
+        return jnp.right_shift(count_ref[inside] + (CHUNK - 1), 8)
 
     total = jnp.int32(0)
     for d in range(STRIPS):
-        total = total + jnp.maximum((count_ref[d] + (CHUNK - 1)) // CHUNK, 1)
+        total = total + jnp.maximum(jnp.right_shift(count_ref[d] + (CHUNK - 1), 8), 1)
 
     copies[0].wait()
     logits = logits_ref[...]
     shifted = jnp.exp(logits - jnp.max(logits, axis=0, keepdims=True))
     prob_ref[...] = (shifted / jnp.sum(shifted, axis=0, keepdims=True)).astype(BF)
-    bins = lax.broadcasted_iota(jnp.int32, (DEPTH, CHUNK), 0)
+    sub8 = lax.broadcasted_iota(jnp.int32, (8, CHUNK), 0)
     slot = lax.broadcasted_iota(jnp.int32, (1, CHUNK), 1)
     copies[1].wait()
     copies[2].wait()
@@ -75,11 +75,18 @@
             pixel = (point & (PIX - 1)).astype(F32)
             hot = onehot_rows(pixel, PIX)
             column = jnp.dot(prob_ref[...], hot, preferred_element_type=F32)
-            bin_id = jnp.broadcast_to(point >> 8, (DEPTH, CHUNK))
-            weight = jnp.sum(jnp.where(bin_id == bins, column, 0.0), axis=0, keepdims=True)
+            bin_id = jnp.broadcast_to(point >> 8, (8, CHUNK))
+            level = [column[8 * g : 8 * g + 8, :] for g in range(DEPTH // 8)]
+            for bit in (8, 16, 32, 64):
+                upper = (bin_id & bit) != 0
+                level = [
+                    jnp.where(upper, level[i + 1], level[i]) if i + 1 < len(level) else level[i]
+                    for i in range(0, len(level), 2)
+                ]
+            weight = jnp.sum(jnp.where((bin_id & 7) == sub8, level[0], 0.0), axis=0, keepdims=True)
             pixel = jnp.where(slot + lane < count_ref[row], pixel, -1.0)
             cell = cell_ref[pl.ds(row, 1), pl.ds(lane, CHUNK)].astype(F32)
-            place = (row & (GROUP - 1)) * ZS + (row >> 3)
+            place = ((row >> 1) & (GROUP - 1)) * ZS + (row & 1) * (ZS // 2) + (row >> 4)
             for ref, value in ((weight_ref, weight), (pixel_ref, pixel), (target_ref, cell)):
                 ref[j, pl.ds(place, 1), :] = value
             last = j + 1 >= chunks_of(strip)
@@ -102,7 +109,6 @@
     for src in range(GROUP):
         slots_ref[src * SLOT_ROWS : (src + 1) * SLOT_ROWS, :] = in_ref[src, :SLOT_ROWS, :].astype(F32)
     acc_ref[...] = jnp.zeros(acc_ref.shape, F32)
-    val_ref[...] = jnp.zeros(val_ref.shape, BF)
 
     rows = ZS * NCH
     lane0 = lax.broadcasted_iota(jnp.int32, (ZS, 128), 1) == 0
@@ -120,42 +126,53 @@
         total = total + jnp.sum(live).astype(jnp.int32)
     word_ref[GROUP] = 0
 
+    def select(slot, b, state):
+        src, z, j = state
+        valid = src < GROUP
+        source = jnp.where(valid, src, 0)
+        row = source * SLOT_ROWS + j * ZS + z
+        weight = slots_ref[pl.ds(row, 1), :]
+        pixel = slots_ref[pl.ds(row + rows, 1), :]
+        hot = onehot_rows(pixel, PIX)
+        feature = jnp.dot(in_ref[source, SLOT_ROWS:ROWS, :], hot, preferred_element_type=F32)
+        val_ref[slot, b] = (feature * weight).astype(BF)
+        item = (row + 2 * rows, jnp.where(valid, z, ZS))
+        chunks = jnp.right_shift(word_ref[jnp.minimum(src, GROUP)], 3 * z) & 7
+        last = j + 1 >= chunks
+        j = jnp.where(last, 0, j + 1)
+        z = jnp.where(last, z + 1, z)
+        wrap = z >= ZS
+        z = jnp.where(wrap, 0, z)
+        src = jnp.where(wrap, src + 1, src)
+        return (src, z, j), item
+
+    def gather(slot, b, item):
+        row, place = item
+        hot = onehot_rows(slots_ref[pl.ds(row, 1), :], CELLS)
+        part = lax.dot_general(
+            val_ref[slot, b], hot, (((1,), (1,)), ((), ())), preferred_element_type=F32
+        )
+        acc_ref[place] = acc_ref[place] + part
+
     def step(it, carry):
-        src, z, j = carry[:3]
-        older = carry[3:]
-        now, before = lax.rem(it, 2), lax.rem(it + 1, 2)
+        state, items = carry
+        before, now = lax.rem(it, 2), lax.rem(it + 1, 2)
         fresh = []
         for b in range(BATCH_B):
-            old_row, old_acc = older[2 * b], older[2 * b + 1]
-            cell = slots_ref[pl.ds(old_row, 1), :]
-            hot = onehot_rows(cell, CELLS)
-            part = lax.dot_general(
-                val_ref[before, b], hot, (((1,), (1,)), ((), ())), preferred_element_type=F32
-            )
-            acc_ref[old_acc] = acc_ref[old_acc] + part
-
-            valid = src < GROUP
-            source = jnp.where(valid, src, 0)
-            row = source * SLOT_ROWS + j * ZS + z
-            weight = slots_ref[pl.ds(row, 1), :]
-            pixel = slots_ref[pl.ds(row + rows, 1), :]
-            hot = onehot_rows(pixel, PIX)
-            feature = jnp.dot(in_ref[source, SLOT_ROWS:ROWS, :], hot, preferred_element_type=F32)
-            val_ref[now, b] = (feature * weight).astype(BF)
-            fresh += [row + 2 * rows, jnp.where(valid, z, ZS)]
-
-            chunks = jnp.right_shift(word_ref[jnp.minimum(src, GROUP)], 3 * z) & 7
-            last = j + 1 >= chunks
-            j = jnp.where(last, 0, j + 1)
-            z = jnp.where(last, z + 1, z)
-            wrap = z >= ZS
-            z = jnp.where(wrap, 0, z)
-            src = jnp.where(wrap, src + 1, src)
-        return (src, z, j, *fresh)
+            gather(before, b, items[b])
+            state, item = select(now, b, state)
+            fresh.append(item)
+        return state, tuple(fresh)
 
     zero = jnp.int32(0)
-    start = (zero, zero, zero) + (zero, jnp.int32(ZS)) * BATCH_B
-    lax.fori_loop(0, (total + BATCH_B - 1) // BATCH_B + 1, step, start)
+    batches = (total + BATCH_B - 1) // BATCH_B
+    state, items = (zero, zero, zero), []
+    for b in range(BATCH_B):
+        state, item = select(0, b, state)
+        items.append(item)
+    _, items = lax.fori_loop(0, batches - 1, step, (state, tuple(items)))
+    for b in range(BATCH_B):
+        gather(lax.rem(batches - 1, 2), b, items[b])
 
     left = lax.broadcasted_iota(jnp.int32, (C // 2, 128), 1) < 64
     for z in range(ZS):
@@ -170,7 +187,7 @@
     parts = []
     for s in range(4):
         total = jnp.zeros((C // 2, 128), F32)
-        for z in range(ZS):
+        for z in range(ZS // 2):
             total = total + in_ref[z * 4 + s].astype(F32)
         parts += [total, pltpu.roll(total, 64, 1)]
     stacked = jnp.concatenate(parts, axis=0)
@@ -235,15 +252,19 @@
 
 def body(context, depth_logits, send_count, slot_point, slot_cell):
     slots = send(send_count[0, 0], depth_logits[0], context[0], slot_point[0, 0], slot_cell[0, 0])
-    slots = lax.all_to_all(slots, ("x", "core"), 0, 0, tiled=True)
-    partials = pool(slots)
-    partials = lax.all_to_all(partials, ("z", "scene"), 0, 0, tiled=True)
+    slots = lax.all_to_all(slots, ("zl", "x"), 0, 0, tiled=True)
+    mine = pool(slots).reshape(2, 2 * ZS, C // 2, 128)
+    theirs = lax.ppermute(mine, "core", [(0, 1), (1, 0)])
+    core = lax.axis_index("core")
+    half = [lax.dynamic_index_in_dim(v, core, 0, keepdims=False).astype(F32) for v in (mine, theirs)]
+    partials = (half[0] + half[1]).astype(BF)
+    partials = lax.all_to_all(partials, ("zh", "scene"), 0, 0, tiled=True)
     return merge(partials)
 
 
 def solution(mesh):
-    split = Mesh(mesh.devices.reshape(8, 4, 2, 4), ("z", "x", "core", "scene"))
-    bev = ("z", "x", "core")
+    split = Mesh(mesh.devices.reshape(4, 2, 4, 2, 4), ("zh", "zl", "x", "core", "scene"))
+    bev = ("zh", "zl", "x", "core")
     return jax.shard_map(
         body,
         mesh=split,
@@ -254,6 +275,6 @@
             P("scene", bev, None, None),
             P("scene", bev, None, None),
         ),
-        out_specs=P(("z", "x", "core", "scene"), None),
+        out_specs=P((*bev, "scene"), None),
         check_vma=False,
     )

time: 54.8 us -> 51.8 us (0.945)
  blocking collectives: 40.6 us -> 36.3 us
  starting transfers between devices: 0 us -> 2.41 us
  Pallas kernels: 13.8 us -> 11.7 us
  waiting for transfers between devices: 0 us -> 1.26 us
    all_to_all x2, blocking collectives: 40.6 us -> 36.3 us  [the longest x1 19.4 us: body(): partials = lax.all_to_all(partials, ('zh', 'scene'), 0, 0, tiled=True)]
    ppermute x0 -> x1, starting transfers between devices: none -> 2.41 us  [body(): theirs = lax.ppermute(mine, 'core', [(0, 1), (1, 0)])]
    pallas_call x1, Pallas kernels: 7.02 us -> 5.63 us  [pool(): pl.pallas_call(pool_kernel, out_shape=jax.ShapeDtypeStruct((ZS * 4, C //...]
    ppermute x0 -> x1, waiting for transfers between devices: none -> 1.26 us  [body(): theirs = lax.ppermute(mine, 'core', [(0, 1), (1, 0)])]
    pallas_call x1, Pallas kernels: 5.93 us -> 5.26 us  [send(): pl.pallas_call(send_kernel, out_shape=pltpu.VMEM((GROUP, ROWS, PIX), BF),...]
  transfers between devices with their start and end apart: 0 -> 1, of which waited for: 0 -> 1; matrix products, arithmetic and copies ran while one was open for 0% -> 0% of each run, Pallas kernels for 0% -> 0%
where the time goes in v3:
time: 51.8 us; the launch traced here: 51.7 us
  blocking collectives  36.3 us (70%)
  Pallas kernels  11.7 us (23%)
  starting transfers between devices  2.41 us (5%)
  waiting for transfers between devices  1.26 us (2%)
    all_to_all x1, blocking collectives, body(): partials = lax.all_to_all(partials, ('zh', 'scene'), 0, 0, tiled=True)  19.4 us
    all_to_all x1, blocking collectives, body(): slots = lax.all_to_all(slots, ('zl', 'x'), 0, 0, tiled=True)  16.9 us
    pallas_call x1, Pallas kernels, pool(): pl.pallas_call(pool_kernel, out_shape=jax.ShapeDtypeStruct((ZS * 4, C //...  5.63 us
    pallas_call x1, Pallas kernels, send(): pl.pallas_call(send_kernel, out_shape=pltpu.VMEM((GROUP, ROWS, PIX), BF),...  5.26 us
    ppermute x1, starting transfers between devices, body(): theirs = lax.ppermute(mine, 'core', [(0, 1), (1, 0)])  2.41 us
    ppermute x1, waiting for transfers between devices, body(): theirs = lax.ppermute(mine, 'core', [(0, 1), (1, 0)])  1.26 us
  transfers between devices with their start and end apart: 1, of which 1 were waited for; matrix products, arithmetic and copies ran while one was open for 0% of the time, Pallas kernels for 0%

profile of v3, /device:TPU:1, one launch (start us, length us, event | category | flops | bytes accessed | tf_op | source)
XLA Modules:
  0.0 51.7 jit_solution(9708182634244833468)
XLA Ops:
  0.0 5.3 %send_slots.1 = bf16[8,176,256]{2,1,0:T(8,128)(2,1)S(1)} custom-call(s32[64]{0:T(128)} %bitcast.14, f32[112,256]{1,0:T(8,128)} %bitcast.12, bf16[80,256]{1,0:T(8,128)(2,1)} %bitcast.13, s32[64,1024]{1,0:T(8,128)} %bitcast.10, s32[64,1024]{1,0:T(8,128)} %bitcast.11), custom_call_target="tpu_custom_call" | custom-call | tf_op jit(solution)/shard_map/send_slots/pallas_call | solution.py:204
  5.3 16.9 %all_to_all.10.in_ref = bf16[8,176,256]{2,1,0:T(8,128)(2,1)S(1)} all-to-all(bf16[8,176,256]{2,1,0:T(8,128)(2,1)S(1)} %send_slots.1), channel_id=1, replica_groups=mesh['zh'=4,'zl'=2,'x'=4,'core'=2,'scene'=4] {'zl','x'}, dimensions={0} | all-to-all | bytes 1441792 | tf_op jit(solution)/shard_map/all_to_all | solution.py:255
  22.2 5.6 %pool_slots.1 = bf16[32,40,128]{2,1,0:T(8,128)(2,1)S(1)} custom-call(bf16[8,176,256]{2,1,0:T(8,128)(2,1)S(1)} %all_to_all.10.in_ref), custom_call_target="tpu_custom_call" | custom-call | tf_op jit(solution)/shard_map/pool_slots/pallas_call | solution.py:226
  27.8 2.4 %collective-permute-start = (bf16[2,16,40,128]{3,2,1,0:T(8,128)(2,1)S(1)}, bf16[2,16,40,128]{3,2,1,0:T(8,128)(2,1)S(1)}, u32[]{:S(2)}, u32[]{:S(2)}) collective-permute-start(bf16[2,16,40,128]{3,2,1,0:T(8,128)(2,1)S(1)} %bitcast.8), channel_id=1, source_target_pairs={{0,4},{4,0},{1,5},{5,1},{2,6},{6,2},{3,7},{7,3},{8,12},{12,8},{9,1... | collective-permute-start | bytes 983048 | tf_op jit(solution)/shard_map/ppermute | solution.py:257
  30.2 1.3 %collective-permute-done = bf16[2,16,40,128]{3,2,1,0:T(8,128)(2,1)S(1)} collective-permute-done((bf16[2,16,40,128]{3,2,1,0:T(8,128)(2,1)S(1)}, bf16[2,16,40,128]{3,2,1,0:T(8,128)(2,1)S(1)}, u32[]{:S(2)}, u32[]{:S(2)}) %collective-permute-start) | collective-permute-done | bytes 327712 | tf_op jit(solution)/shard_map/ppermute | solution.py:257
  31.5 19.4 %all_to_all.11.in_ref = bf16[16,40,128]{2,1,0:T(8,128)(2,1)S(1)} all-to-all(bf16[16,40,128]{2,1,0:T(8,128)(2,1)S(1)} %fusion), channel_id=1, replica_groups=mesh['zh'=4,'zl'=2,'x'=4,'core'=2,'scene'=4] {'zh','scene'}, dimensions={0} | all-to-all | bytes 327680 | tf_op jit(solution)/shard_map/all_to_all | solution.py:261
  50.9 0.8 %merge_parts.1 = bf16[64,320]{1,0:T(8,128)(2,1)} custom-call(bf16[16,40,128]{2,1,0:T(8,128)(2,1)S(1)} %all_to_all.11.in_ref), custom_call_target="tpu_custom_call" | custom-call | tf_op jit(solution)/shard_map/merge_parts/pallas_call | solution.py:243
  (1 shorter events, 0.0 us)
Async XLA Ops:
  27.8 3.7 %collective-permute-start = (bf16[2,16,40,128]{3,2,1,0:T(8,128)(2,1)S(1)}, bf16[2,16,40,128]{3,2,1,0:T(8,128)(2,1)S(1)}, u32[]{:S(2)}, u32[]{:S(2)}) collective-permute-start(bf16[2,16,40,128]{3,2,1,0:T(8,128)(2,1)S(1)} %bitcast.8), channel_id=1, source_target_pairs={{0,4},{4,0},{1,5},{5,1},{2,6},{6,2},{3,7},{7,3},{8,12},{12,8},{9,1... | collective-permute-start | bytes 983048 | tf_op jit(solution)/shard_map/ppermute | solution.py:257

commit v4 on v3

--- a/solution.py
+++ b/solution.py
@@ -13,11 +13,12 @@
 CAP = 1024
 CHUNK = 256
 NCH = CAP // CHUNK
+TILES = CAP // 128
 GROUP = 8
 ZS = 8
 SLOT_ROWS = 3 * ZS * NCH
 ROWS = SLOT_ROWS + C
-BATCH_A = 56
+BATCH_A = 50
 BATCH_B = 28
 
 BF = jnp.bfloat16
@@ -38,10 +39,11 @@
 
 
 def send_kernel(
-    count_ref, logits_hbm, ctx_hbm, point_hbm, cell_hbm, out_ref,
-    logits_ref, ctx_ref, point_ref, cell_ref, prob_ref, weight_ref, pixel_ref, target_ref, sems,
+    count_hbm, logits_hbm, ctx_hbm, point_hbm, cell_hbm, out_ref,
+    count_ref, logits_ref, ctx_ref, raw_point_ref, raw_cell_ref, point_ref, cell_ref, prob_ref, weight_ref, pixel_ref, target_ref, sems,
 ):
-    pairs = ((logits_hbm, logits_ref), (point_hbm, point_ref), (cell_hbm, cell_ref), (ctx_hbm, ctx_ref))
+    pairs = [(count_hbm, count_ref), (logits_hbm, logits_ref), (ctx_hbm, ctx_ref)]
+    pairs += [(point_hbm, raw_point_ref), (cell_hbm, raw_cell_ref)]
     copies = [pltpu.make_async_copy(src, dst, sems.at[i]) for i, (src, dst) in enumerate(pairs)]
     for copy in copies:
         copy.start()
@@ -49,59 +51,73 @@
     pixel_ref[...] = jnp.full(pixel_ref.shape, -1.0, F32)
     target_ref[...] = jnp.zeros(target_ref.shape, F32)
 
-    def chunks_of(strip):
-        inside = jnp.minimum(strip, STRIPS - 1)
-        return jnp.right_shift(count_ref[inside] + (CHUNK - 1), 8)
-
+    def pieces_of(count):
+        return jnp.maximum(jnp.right_shift(count + 127, 7), 1)
+
+    copies[0].wait()
     total = jnp.int32(0)
     for d in range(STRIPS):
-        total = total + jnp.maximum(jnp.right_shift(count_ref[d] + (CHUNK - 1), 8), 1)
-
-    copies[0].wait()
+        total = total + pieces_of(count_ref[d])
+
+    copies[1].wait()
     logits = logits_ref[...]
     shifted = jnp.exp(logits - jnp.max(logits, axis=0, keepdims=True))
     prob_ref[...] = (shifted / jnp.sum(shifted, axis=0, keepdims=True)).astype(BF)
-    sub8 = lax.broadcasted_iota(jnp.int32, (8, CHUNK), 0)
-    slot = lax.broadcasted_iota(jnp.int32, (1, CHUNK), 1)
-    copies[1].wait()
-    copies[2].wait()
+    sub8 = lax.broadcasted_iota(jnp.int32, (8, 128), 0)
+    slot = lax.broadcasted_iota(jnp.int32, (1, 128), 1)
+    for copy in copies[2:]:
+        copy.wait()
+    for t in range(TILES):
+        point_ref[t] = raw_point_ref[:, t * 128 : (t + 1) * 128]
+        cell_ref[t] = raw_cell_ref[:, t * 128 : (t + 1) * 128]
 
     def step(_, carry):
         strip, j = carry
         for _ in range(BATCH_A):
-            row = jnp.minimum(strip, STRIPS - 1)
-            lane = pl.multiple_of(j * CHUNK, CHUNK)
-            point = point_ref[pl.ds(row, 1), pl.ds(lane, CHUNK)]
-            pixel = (point & (PIX - 1)).astype(F32)
-            hot = onehot_rows(pixel, PIX)
-            column = jnp.dot(prob_ref[...], hot, preferred_element_type=F32)
-            bin_id = jnp.broadcast_to(point >> 8, (8, CHUNK))
-            level = [column[8 * g : 8 * g + 8, :] for g in range(DEPTH // 8)]
-            for bit in (8, 16, 32, 64):
-                upper = (bin_id & bit) != 0
-                level = [
-                    jnp.where(upper, level[i + 1], level[i]) if i + 1 < len(level) else level[i]
-                    for i in range(0, len(level), 2)
-                ]
-            weight = jnp.sum(jnp.where((bin_id & 7) == sub8, level[0], 0.0), axis=0, keepdims=True)
-            pixel = jnp.where(slot + lane < count_ref[row], pixel, -1.0)
-            cell = cell_ref[pl.ds(row, 1), pl.ds(lane, CHUNK)].astype(F32)
-            place = ((row >> 1) & (GROUP - 1)) * ZS + (row & 1) * (ZS // 2) + (row >> 4)
-            for ref, value in ((weight_ref, weight), (pixel_ref, pixel), (target_ref, cell)):
-                ref[j, pl.ds(place, 1), :] = value
-            last = j + 1 >= chunks_of(strip)
-            strip = jnp.where(last, strip + 1, strip)
-            j = jnp.where(last, 0, j + 1)
+            rows, hots = [], []
+            for _ in range(2):
+                row = jnp.minimum(strip, STRIPS - 1)
+                count = count_ref[row]
+                point = point_ref[j, pl.ds(row, 1), :]
+                rows.append((row, j, count, point))
+                hots.append(onehot_rows((point & (PIX - 1)).astype(F32), PIX))
+                last = j + 1 >= pieces_of(count)
+                strip = jnp.where(last, strip + 1, strip)
+                j = jnp.where(last, 0, j + 1)
+            hot = jnp.concatenate(hots, axis=1)
+            columns = jnp.dot(prob_ref[...], hot, preferred_element_type=F32)
+            for half, (row, piece, count, point) in enumerate(rows):
+                bin_id = jnp.broadcast_to(jnp.right_shift(point, 8), (8, 128))
+                column = columns[:, half * 128 : (half + 1) * 128]
+                level = [column[8 * g : 8 * g + 8, :] for g in range(DEPTH // 8)]
+                for bit in (8, 16, 32, 64):
+                    upper = (bin_id & bit) != 0
+                    level = [
+                        jnp.where(upper, level[i + 1], level[i]) if i + 1 < len(level) else level[i]
+                        for i in range(0, len(level), 2)
+                    ]
+                weight = jnp.sum(jnp.where((bin_id & 7) == sub8, level[0], 0.0), axis=0, keepdims=True)
+                pixel = jnp.where(slot + piece * 128 < count, point & (PIX - 1), -1).astype(F32)
+                cell = cell_ref[piece, pl.ds(row, 1), :].astype(F32)
+                inside = jnp.right_shift(row, 1)
+                place = (inside & (GROUP - 1)) * ZS + (row & 1) * (ZS // 2) + jnp.right_shift(row, 4)
+                for ref, value in ((weight_ref, weight), (pixel_ref, pixel), (target_ref, cell)):
+                    ref[piece, pl.ds(place, 1), :] = value
         return strip, j
 
-    lax.fori_loop(0, (total + BATCH_A - 1) // BATCH_A, step, (jnp.int32(0), jnp.int32(0)))
-
-    copies[3].wait()
+    steps = (total + 2 * BATCH_A - 1) // (2 * BATCH_A)
+    lax.fori_loop(0, steps, step, (jnp.int32(0), jnp.int32(0)))
+
     context = ctx_ref[...]
     for dest in range(GROUP):
         for kind, ref in enumerate((weight_ref, pixel_ref, target_ref)):
-            stacked = jnp.concatenate([ref[i, dest * ZS : (dest + 1) * ZS, :] for i in range(NCH)], axis=0)
-            out_ref[dest, kind * ZS * NCH : (kind + 1) * ZS * NCH, :] = stacked.astype(BF)
+            for half in range(2):
+                stacked = jnp.concatenate(
+                    [ref[2 * i + half, dest * ZS : (dest + 1) * ZS, :] for i in range(NCH)], axis=0
+                )
+                out_ref[
+                    dest, kind * ZS * NCH : (kind + 1) * ZS * NCH, half * 128 : (half + 1) * 128
+                ] = stacked.astype(BF)
         out_ref[dest, SLOT_ROWS:ROWS, :] = context
 
 
@@ -204,18 +220,21 @@
     return pl.pallas_call(
         send_kernel,
         out_shape=pltpu.VMEM((GROUP, ROWS, PIX), BF),
-        in_specs=[SMEM, HBM, HBM, HBM, HBM],
+        in_specs=[HBM, HBM, HBM, HBM, HBM],
         out_specs=VMEM,
         scratch_shapes=[
+            pltpu.SMEM((STRIPS,), jnp.int32),
             pltpu.VMEM((DEPTH, PIX), F32),
             pltpu.VMEM((C, PIX), BF),
             pltpu.VMEM((STRIPS, CAP), jnp.int32),
             pltpu.VMEM((STRIPS, CAP), jnp.int32),
+            pltpu.VMEM((TILES, STRIPS, 128), jnp.int32),
+            pltpu.VMEM((TILES, STRIPS, 128), jnp.int32),
             pltpu.VMEM((DEPTH, PIX), BF),
-            pltpu.VMEM((NCH, STRIPS, CHUNK), F32),
-            pltpu.VMEM((NCH, STRIPS, CHUNK), F32),
-            pltpu.VMEM((NCH, STRIPS, CHUNK), F32),
-            pltpu.SemaphoreType.DMA((4,)),
+            pltpu.VMEM((TILES, STRIPS, 128), F32),
+            pltpu.VMEM((TILES, STRIPS, 128), F32),
+            pltpu.VMEM((TILES, STRIPS, 128), F32),
+            pltpu.SemaphoreType.DMA((5,)),
         ],
         compiler_params=pltpu.CompilerParams(vmem_limit_bytes=67043328 - 800 * 1024),
         name="send_slots",

time: 51.8 us -> 51.2 us (0.988)
  Pallas kernels: 11.7 us -> 11 us
    pallas_call x1, Pallas kernels: 5.26 us -> 4.59 us  [send(): pl.pallas_call(send_kernel, out_shape=pltpu.VMEM((GROUP, ROWS, PIX), BF),...]
where the time goes in v4:
time: 51.2 us; the launch traced here: 51 us
  blocking collectives  36.3 us (71%)
  Pallas kernels  11 us (21%)
  starting transfers between devices  2.41 us (5%)
  waiting for transfers between devices  1.26 us (2%)
    all_to_all x1, blocking collectives, body(): partials = lax.all_to_all(partials, ('zh', 'scene'), 0, 0, tiled=True)  19.4 us
    all_to_all x1, blocking collectives, body(): slots = lax.all_to_all(slots, ('zl', 'x'), 0, 0, tiled=True)  16.9 us
    pallas_call x1, Pallas kernels, pool(): pl.pallas_call(pool_kernel, out_shape=jax.ShapeDtypeStruct((ZS * 4, C //...  5.62 us
    pallas_call x1, Pallas kernels, send(): pl.pallas_call(send_kernel, out_shape=pltpu.VMEM((GROUP, ROWS, PIX), BF),...  4.59 us
    ppermute x1, starting transfers between devices, body(): theirs = lax.ppermute(mine, 'core', [(0, 1), (1, 0)])  2.41 us
    ppermute x1, waiting for transfers between devices, body(): theirs = lax.ppermute(mine, 'core', [(0, 1), (1, 0)])  1.26 us
  transfers between devices with their start and end apart: 1, of which 1 were waited for; matrix products, arithmetic and copies ran while one was open for 0% of the time, Pallas kernels for 0%

profile of v4, /device:TPU:1, one launch (start us, length us, event | category | flops | bytes accessed | tf_op | source)
XLA Modules:
  0.0 51.0 jit_solution(14366315425695163692)
XLA Ops:
  0.0 4.6 %send_slots.1 = bf16[8,176,256]{2,1,0:T(8,128)(2,1)S(1)} custom-call(s32[64]{0:T(128)} %bitcast.14, f32[112,256]{1,0:T(8,128)} %bitcast.12, bf16[80,256]{1,0:T(8,128)(2,1)} %bitcast.13, s32[64,1024]{1,0:T(8,128)} %bitcast.10, s32[64,1024]{1,0:T(8,128)} %bitcast.11), custom_call_target="tpu_custom_call" | custom-call | tf_op jit(solution)/shard_map/send_slots/pallas_call | solution.py:220
  4.6 16.9 %all_to_all.10.in_ref = bf16[8,176,256]{2,1,0:T(8,128)(2,1)S(1)} all-to-all(bf16[8,176,256]{2,1,0:T(8,128)(2,1)S(1)} %send_slots.1), channel_id=1, replica_groups=mesh['zh'=4,'zl'=2,'x'=4,'core'=2,'scene'=4] {'zl','x'}, dimensions={0} | all-to-all | bytes 1441792 | tf_op jit(solution)/shard_map/all_to_all | solution.py:274
  21.5 5.6 %pool_slots.1 = bf16[32,40,128]{2,1,0:T(8,128)(2,1)S(1)} custom-call(bf16[8,176,256]{2,1,0:T(8,128)(2,1)S(1)} %all_to_all.10.in_ref), custom_call_target="tpu_custom_call" | custom-call | tf_op jit(solution)/shard_map/pool_slots/pallas_call | solution.py:245
  27.1 2.4 %collective-permute-start = (bf16[2,16,40,128]{3,2,1,0:T(8,128)(2,1)S(1)}, bf16[2,16,40,128]{3,2,1,0:T(8,128)(2,1)S(1)}, u32[]{:S(2)}, u32[]{:S(2)}) collective-permute-start(bf16[2,16,40,128]{3,2,1,0:T(8,128)(2,1)S(1)} %bitcast.8), channel_id=1, source_target_pairs={{0,4},{4,0},{1,5},{5,1},{2,6},{6,2},{3,7},{7,3},{8,12},{12,8},{9,1... | collective-permute-start | bytes 983048 | tf_op jit(solution)/shard_map/ppermute | solution.py:276
  29.5 1.3 %collective-permute-done = bf16[2,16,40,128]{3,2,1,0:T(8,128)(2,1)S(1)} collective-permute-done((bf16[2,16,40,128]{3,2,1,0:T(8,128)(2,1)S(1)}, bf16[2,16,40,128]{3,2,1,0:T(8,128)(2,1)S(1)}, u32[]{:S(2)}, u32[]{:S(2)}) %collective-permute-start) | collective-permute-done | bytes 327712 | tf_op jit(solution)/shard_map/ppermute | solution.py:276
  30.8 19.4 %all_to_all.11.in_ref = bf16[16,40,128]{2,1,0:T(8,128)(2,1)S(1)} all-to-all(bf16[16,40,128]{2,1,0:T(8,128)(2,1)S(1)} %fusion), channel_id=1, replica_groups=mesh['zh'=4,'zl'=2,'x'=4,'core'=2,'scene'=4] {'zh','scene'}, dimensions={0} | all-to-all | bytes 327680 | tf_op jit(solution)/shard_map/all_to_all | solution.py:280
  50.2 0.8 %merge_parts.1 = bf16[64,320]{1,0:T(8,128)(2,1)} custom-call(bf16[16,40,128]{2,1,0:T(8,128)(2,1)S(1)} %all_to_all.11.in_ref), custom_call_target="tpu_custom_call" | custom-call | tf_op jit(solution)/shard_map/merge_parts/pallas_call | solution.py:262
  (1 shorter events, 0.0 us)
Async XLA Ops:
  27.1 3.7 %collective-permute-start = (bf16[2,16,40,128]{3,2,1,0:T(8,128)(2,1)S(1)}, bf16[2,16,40,128]{3,2,1,0:T(8,128)(2,1)S(1)}, u32[]{:S(2)}, u32[]{:S(2)}) collective-permute-start(bf16[2,16,40,128]{3,2,1,0:T(8,128)(2,1)S(1)} %bitcast.8), channel_id=1, source_target_pairs={{0,4},{4,0},{1,5},{5,1},{2,6},{6,2},{3,7},{7,3},{8,12},{12,8},{9,1... | collective-permute-start | bytes 983048 | tf_op jit(solution)/shard_map/ppermute | solution.py:276

commit v5 on v4

--- a/solution.py
+++ b/solution.py
@@ -1,3 +1,5 @@
+import functools
+
 import jax
 import jax.numpy as jnp
 from jax import lax
@@ -18,8 +20,9 @@
 ZS = 8
 SLOT_ROWS = 3 * ZS * NCH
 ROWS = SLOT_ROWS + C
-BATCH_A = 50
-BATCH_B = 28
+BATCH_A = 44
+BATCH_B = 25
+BATCH_OWN = 7
 
 BF = jnp.bfloat16
 F32 = jnp.float32
@@ -38,8 +41,12 @@
     ).astype(jnp.float8_e4m3fn)
 
 
+def own_place():
+    return lax.axis_index(("zl", "x"))
+
+
 def send_kernel(
-    count_hbm, logits_hbm, ctx_hbm, point_hbm, cell_hbm, out_ref,
+    peers, count_hbm, logits_hbm, ctx_hbm, point_hbm, cell_hbm, out_ref,
     count_ref, logits_ref, ctx_ref, raw_point_ref, raw_cell_ref, point_ref, cell_ref, prob_ref, weight_ref, pixel_ref, target_ref, sems,
 ):
     pairs = [(count_hbm, count_ref), (logits_hbm, logits_ref), (ctx_hbm, ctx_ref)]
@@ -54,10 +61,18 @@
     def pieces_of(count):
         return jnp.maximum(jnp.right_shift(count + 127, 7), 1)
 
+    own = own_place()
+    first = 1 if peers > 1 else 0
+    strips = peers * ZS
+
+    def row_of(strip):
+        dest = (own + first + jnp.right_shift(strip, 3)) & (GROUP - 1)
+        return jnp.left_shift(strip & 3, 4) + 2 * dest + (jnp.right_shift(strip, 2) & 1)
+
     copies[0].wait()
     total = jnp.int32(0)
-    for d in range(STRIPS):
-        total = total + pieces_of(count_ref[d])
+    for d in range(strips):
+        total = total + pieces_of(count_ref[row_of(jnp.int32(d))])
 
     copies[1].wait()
     logits = logits_ref[...]
@@ -73,10 +88,10 @@
 
     def step(_, carry):
         strip, j = carry
-        for _ in range(BATCH_A):
+        for _ in range(BATCH_A if peers > 1 else BATCH_OWN):
             rows, hots = [], []
             for _ in range(2):
-                row = jnp.minimum(strip, STRIPS - 1)
+                row = row_of(jnp.minimum(strip, strips - 1))
                 count = count_ref[row]
                 point = point_ref[j, pl.ds(row, 1), :]
                 rows.append((row, j, count, point))
@@ -100,16 +115,19 @@
                 pixel = jnp.where(slot + piece * 128 < count, point & (PIX - 1), -1).astype(F32)
                 cell = cell_ref[piece, pl.ds(row, 1), :].astype(F32)
                 inside = jnp.right_shift(row, 1)
-                place = (inside & (GROUP - 1)) * ZS + (row & 1) * (ZS // 2) + jnp.right_shift(row, 4)
+                place = (row & 1) * (ZS // 2) + jnp.right_shift(row, 4)
+                if peers > 1:
+                    place = place + (inside & (GROUP - 1)) * ZS
                 for ref, value in ((weight_ref, weight), (pixel_ref, pixel), (target_ref, cell)):
                     ref[piece, pl.ds(place, 1), :] = value
         return strip, j
 
-    steps = (total + 2 * BATCH_A - 1) // (2 * BATCH_A)
+    batch = 2 * (BATCH_A if peers > 1 else BATCH_OWN)
+    steps = (total + batch - 1) // batch
     lax.fori_loop(0, steps, step, (jnp.int32(0), jnp.int32(0)))
 
     context = ctx_ref[...]
-    for dest in range(GROUP):
+    for dest in range(GROUP if peers > 1 else 1):
         for kind, ref in enumerate((weight_ref, pixel_ref, target_ref)):
             for half in range(2):
                 stacked = jnp.concatenate(
@@ -121,16 +139,26 @@
         out_ref[dest, SLOT_ROWS:ROWS, :] = context
 
 
-def pool_kernel(in_ref, out_ref, slots_ref, acc_ref, val_ref, word_ref):
-    for src in range(GROUP):
+def pool_kernel(in_ref, *refs):
+    peers = in_ref.shape[0]
+    if peers > 1:
+        seed_ref, out_ref, slots_ref, acc_ref, val_ref, word_ref = refs
+        acc_ref[...] = seed_ref[...]
+        batch = BATCH_B
+    else:
+        acc_ref, slots_ref, val_ref, word_ref = refs
+        acc_ref[...] = jnp.zeros(acc_ref.shape, F32)
+        batch = BATCH_OWN
+    own = own_place()
+    used = GROUP - 1 if peers > 1 else 1
+    for src in range(peers):
         slots_ref[src * SLOT_ROWS : (src + 1) * SLOT_ROWS, :] = in_ref[src, :SLOT_ROWS, :].astype(F32)
-    acc_ref[...] = jnp.zeros(acc_ref.shape, F32)
 
     rows = ZS * NCH
     lane0 = lax.broadcasted_iota(jnp.int32, (ZS, 128), 1) == 0
     digit = jnp.left_shift(1, 3 * lax.broadcasted_iota(jnp.int32, (ZS, 128), 0)).astype(F32)
     total = jnp.int32(0)
-    for src in range(GROUP):
+    for src in range(peers):
         live = jnp.zeros((ZS, 128), F32)
         for j in range(NCH):
             first = slots_ref[src * SLOT_ROWS + rows + j * ZS : src * SLOT_ROWS + rows + (j + 1) * ZS, :128]
@@ -140,12 +168,15 @@
             live = live + jnp.where(lane0 & on, 1.0, 0.0)
         word_ref[src] = jnp.sum(live * digit).astype(jnp.int32)
         total = total + jnp.sum(live).astype(jnp.int32)
-    word_ref[GROUP] = 0
+    if peers > 1:
+        total = total - ZS
 
     def select(slot, b, state):
         src, z, j = state
-        valid = src < GROUP
+        valid = src < used
         source = jnp.where(valid, src, 0)
+        if peers > 1:
+            source = (own + 1 + source) & (GROUP - 1)
         row = source * SLOT_ROWS + j * ZS + z
         weight = slots_ref[pl.ds(row, 1), :]
         pixel = slots_ref[pl.ds(row + rows, 1), :]
@@ -153,7 +184,7 @@
         feature = jnp.dot(in_ref[source, SLOT_ROWS:ROWS, :], hot, preferred_element_type=F32)
         val_ref[slot, b] = (feature * weight).astype(BF)
         item = (row + 2 * rows, jnp.where(valid, z, ZS))
-        chunks = jnp.right_shift(word_ref[jnp.minimum(src, GROUP)], 3 * z) & 7
+        chunks = jnp.right_shift(word_ref[source], 3 * z) & 7
         last = j + 1 >= chunks
         j = jnp.where(last, 0, j + 1)
         z = jnp.where(last, z + 1, z)
@@ -174,22 +205,24 @@
         state, items = carry
         before, now = lax.rem(it, 2), lax.rem(it + 1, 2)
         fresh = []
-        for b in range(BATCH_B):
+        for b in range(batch):
             gather(before, b, items[b])
             state, item = select(now, b, state)
             fresh.append(item)
         return state, tuple(fresh)
 
     zero = jnp.int32(0)
-    batches = (total + BATCH_B - 1) // BATCH_B
+    batches = (total + batch - 1) // batch
     state, items = (zero, zero, zero), []
-    for b in range(BATCH_B):
+    for b in range(batch):
         state, item = select(0, b, state)
         items.append(item)
     _, items = lax.fori_loop(0, batches - 1, step, (state, tuple(items)))
-    for b in range(BATCH_B):
+    for b in range(batch):
         gather(lax.rem(batches - 1, 2), b, items[b])
 
+    if peers == 1:
+        return
     left = lax.broadcasted_iota(jnp.int32, (C // 2, 128), 1) < 64
     for z in range(ZS):
         for t in range(2):
@@ -210,16 +243,21 @@
     out_ref[...] = stacked.T[:64, :].astype(BF)
 
 
+SEND_LIMIT = 67043328 - 3 * 1024 * 1024
 PARAMS = pltpu.CompilerParams(vmem_limit_bytes=12 * 1024 * 1024)
 VMEM = pl.BlockSpec(memory_space=pltpu.VMEM)
 HBM = pl.BlockSpec(memory_space=pltpu.HBM)
 SMEM = pl.BlockSpec(memory_space=pltpu.SMEM)
 
 
-def send(counts, logits, context, points, cells):
+COST = pl.CostEstimate(flops=2 * 10**9, bytes_accessed=10**6, transcendentals=0)
+
+
+def send(peers, counts, logits, context, points, cells):
+    dests = GROUP if peers > 1 else 1
     return pl.pallas_call(
-        send_kernel,
-        out_shape=pltpu.VMEM((GROUP, ROWS, PIX), BF),
+        functools.partial(send_kernel, peers),
+        out_shape=pltpu.VMEM((dests, ROWS, PIX), BF),
         in_specs=[HBM, HBM, HBM, HBM, HBM],
         out_specs=VMEM,
         scratch_shapes=[
@@ -231,31 +269,35 @@
             pltpu.VMEM((TILES, STRIPS, 128), jnp.int32),
             pltpu.VMEM((TILES, STRIPS, 128), jnp.int32),
             pltpu.VMEM((DEPTH, PIX), BF),
-            pltpu.VMEM((TILES, STRIPS, 128), F32),
-            pltpu.VMEM((TILES, STRIPS, 128), F32),
-            pltpu.VMEM((TILES, STRIPS, 128), F32),
+            pltpu.VMEM((TILES, dests * ZS, 128), F32),
+            pltpu.VMEM((TILES, dests * ZS, 128), F32),
+            pltpu.VMEM((TILES, dests * ZS, 128), F32),
             pltpu.SemaphoreType.DMA((5,)),
         ],
-        compiler_params=pltpu.CompilerParams(vmem_limit_bytes=67043328 - 800 * 1024),
+        compiler_params=pltpu.CompilerParams(vmem_limit_bytes=SEND_LIMIT),
+        cost_estimate=COST,
         name="send_slots",
     )(counts, logits, context, points, cells)
 
 
-def pool(slots):
+def pool(slots, *seed):
+    peers = slots.shape[0]
+    batch = BATCH_B if seed else BATCH_OWN
+    sums = (ZS + 1, C, CELLS)
+    scratch = [pltpu.VMEM((peers * SLOT_ROWS, CHUNK), F32)]
+    if seed:
+        scratch.append(pltpu.VMEM(sums, F32))
     return pl.pallas_call(
         pool_kernel,
-        out_shape=jax.ShapeDtypeStruct((ZS * 4, C // 2, 128), BF),
-        in_specs=[VMEM],
+        out_shape=jax.ShapeDtypeStruct((ZS * 4, C // 2, 128), BF) if seed else jax.ShapeDtypeStruct(sums, F32),
+        in_specs=[VMEM] * (1 + len(seed)),
         out_specs=VMEM,
-        scratch_shapes=[
-            pltpu.VMEM((GROUP * SLOT_ROWS, CHUNK), F32),
-            pltpu.VMEM((ZS + 1, C, CELLS), F32),
-            pltpu.VMEM((2, BATCH_B, C, CHUNK), BF),
-            pltpu.SMEM((GROUP + 1,), jnp.int32),
-        ],
+        scratch_shapes=scratch
+        + [pltpu.VMEM((2, batch, C, CHUNK), BF), pltpu.SMEM((GROUP + 1,), jnp.int32)],
         compiler_params=PARAMS,
+        cost_estimate=COST,
         name="pool_slots",
-    )(slots)
+    )(slots, *seed)
 
 
 def merge(partials):
@@ -270,9 +312,10 @@
 
 
 def body(context, depth_logits, send_count, slot_point, slot_cell):
-    slots = send(send_count[0, 0], depth_logits[0], context[0], slot_point[0, 0], slot_cell[0, 0])
-    slots = lax.all_to_all(slots, ("zl", "x"), 0, 0, tiled=True)
-    mine = pool(slots).reshape(2, 2 * ZS, C // 2, 128)
+    block = (send_count[0, 0], depth_logits[0], context[0], slot_point[0, 0], slot_cell[0, 0])
+    slots = lax.all_to_all(send(GROUP - 1, *block), ("zl", "x"), 0, 0, tiled=True)
+    seed = pool(send(1, *block))
+    mine = pool(slots, seed).reshape(2, 2 * ZS, C // 2, 128)
     theirs = lax.ppermute(mine, "core", [(0, 1), (1, 0)])
     core = lax.axis_index("core")
     half = [lax.dynamic_index_in_dim(v, core, 0, keepdims=False).astype(F32) for v in (mine, theirs)]

time: 51.2 us -> 51.1 us (level); the launches traced: 51 us -> 50.2 us
  blocking collectives: 36.3 us -> 19.3 us
  waiting for transfers between devices: 1.26 us -> 8.5 us
  starting transfers between devices: 2.41 us -> 8.27 us
  Pallas kernels: 11 us -> 14 us
    all_to_all x1 -> x0, blocking collectives: 16.9 us -> none  [body(): slots = lax.all_to_all(slots, ('zl', 'x'), 0, 0, tiled=True)]
    all_to_all x0 -> x1, waiting for transfers between devices: none -> 7.24 us  [body(): lax.all_to_all(send(GROUP - 1, *block), ('zl', 'x'), 0, 0, tiled=True)]
    all_to_all x0 -> x1, starting transfers between devices: none -> 6.21 us  [body(): lax.all_to_all(send(GROUP - 1, *block), ('zl', 'x'), 0, 0, tiled=True)]
    pallas_call x1 -> x2, Pallas kernels: 4.59 us -> 7.04 us  [send(): pl.pallas_call(functools.partial(send_kernel, peers), out_shape=pltpu.VME...]
    pallas_call x1 -> x2, Pallas kernels: 5.62 us -> 6.2 us  [pool(): pl.pallas_call(pool_kernel, out_shape=jax.ShapeDtypeStruct((ZS * 4, C //...]
  transfers between devices with their start and end apart: 1 -> 2, of which waited for: 1 -> 2; matrix products, arithmetic and copies ran while one was open for 0% -> 0% of each run, Pallas kernels for 0% -> 6%
where the time goes in v5:
time: 51.1 us; the launch traced here: 50.2 us
  blocking collectives  19.3 us (38%)
  Pallas kernels  14 us (27%)
  waiting for transfers between devices  8.5 us (17%)
  starting transfers between devices  8.27 us (16%)
    all_to_all x1, blocking collectives, body(): partials = lax.all_to_all(partials, ('zh', 'scene'), 0, 0, tiled=True)  19.3 us
    all_to_all x1, waiting for transfers between devices, body(): lax.all_to_all(send(GROUP - 1, *block), ('zl', 'x'), 0, 0, tiled=True)  7.24 us
    pallas_call x2, Pallas kernels, send(): pl.pallas_call(functools.partial(send_kernel, peers), out_shape=pltpu.VME...  7.04 us
    all_to_all x1, starting transfers between devices, body(): lax.all_to_all(send(GROUP - 1, *block), ('zl', 'x'), 0, 0, tiled=True)  6.21 us
    pallas_call x2, Pallas kernels, pool(): pl.pallas_call(pool_kernel, out_shape=jax.ShapeDtypeStruct((ZS * 4, C //...  6.2 us
    ppermute x1, starting transfers between devices, body(): theirs = lax.ppermute(mine, 'core', [(0, 1), (1, 0)])  2.06 us
    ppermute x1, waiting for transfers between devices, body(): theirs = lax.ppermute(mine, 'core', [(0, 1), (1, 0)])  1.26 us
  transfers between devices with their start and end apart: 2, of which 2 were waited for; matrix products, arithmetic and copies ran while one was open for 0% of the time, Pallas kernels for 6%

profile of v5, /device:TPU:1, one launch (start us, length us, event | category | flops | bytes accessed | tf_op | source)
XLA Modules:
  0.0 50.2 jit_solution(12368662489848833615)
XLA Ops:
  0.0 5.1 %send_slots.2 = bf16[8,176,256]{2,1,0:T(8,128)(2,1)} custom-call(s32[64]{0:T(128)} %bitcast.18, f32[112,256]{1,0:T(8,128)} %bitcast.14, bf16[80,256]{1,0:T(8,128)(2,1)} %bitcast.16, s32[64,1024]{1,0:T(8,128)} %bitcast.10, s32[64,1024]{1,0:T(8,128)} %bitcast.12), custom_call_target="tpu_custom_call" | custom-call | flops 2000000000 | bytes 1000000 | tf_op jit(solution)/shard_map/send_slots/pallas_call | solution.py:258
  5.1 6.2 %all-to-all-start = ((bf16[8,176,256]{2,1,0:T(8,128)(2,1)}), bf16[8,176,256]{2,1,0:T(8,128)(2,1)S(1)}, u32[]{:S(2)}, u32[]{:S(2)}) async-start(bf16[8,176,256]{2,1,0:T(8,128)(2,1)} %send_slots.2), calls=%async_computation | async-start | bytes 1441792 | tf_op jit(solution)/shard_map/all_to_all | solution.py:316
  11.3 1.9 %send_slots.3.in_ref = bf16[1,176,256]{2,1,0:T(8,128)(2,1)S(1)} custom-call(s32[64]{0:T(128)} %bitcast.19, f32[112,256]{1,0:T(8,128)} %bitcast.15, bf16[80,256]{1,0:T(8,128)(2,1)} %bitcast.17, s32[64,1024]{1,0:T(8,128)} %bitcast.11, s32[64,1024]{1,0:T(8,128)} %bitcast.13), custom_call_target="tpu_custom_call" | custom-call | flops 2000000000 | bytes 1000000 | tf_op jit(solution)/shard_map/send_slots/pallas_call | solution.py:258
  13.3 1.1 %pool_slots.2.refs_0_ = f32[9,80,256]{2,1,0:T(8,128)S(1)} custom-call(bf16[1,176,256]{2,1,0:T(8,128)(2,1)S(1)} %send_slots.3.in_ref), custom_call_target="tpu_custom_call" | custom-call | flops 2000000000 | bytes 1000000 | tf_op jit(solution)/shard_map/pool_slots/pallas_call | solution.py:290
  14.3 7.2 %all-to-all-done.in_ref = bf16[8,176,256]{2,1,0:T(8,128)(2,1)S(1)} async-done(((bf16[8,176,256]{2,1,0:T(8,128)(2,1)}), bf16[8,176,256]{2,1,0:T(8,128)(2,1)S(1)}, u32[]{:S(2)}, u32[]{:S(2)}) %all-to-all-start) | async-done | bytes 720928 | tf_op jit(solution)/shard_map/all_to_all | solution.py:316
  21.6 5.1 %pool_slots.3 = bf16[32,40,128]{2,1,0:T(8,128)(2,1)S(1)} custom-call(bf16[8,176,256]{2,1,0:T(8,128)(2,1)S(1)} %all-to-all-done.in_ref, f32[9,80,256]{2,1,0:T(8,128)S(1)} %pool_slots.2.refs_0_), custom_call_target="tpu_custom_call" | custom-call | flops 2000000000 | bytes 1000000 | tf_op jit(solution)/shard_map/pool_slots/pallas_call | solution.py:290
  26.7 2.1 %collective-permute-start = (bf16[2,16,40,128]{3,2,1,0:T(8,128)(2,1)S(1)}, bf16[2,16,40,128]{3,2,1,0:T(8,128)(2,1)S(1)}, u32[]{:S(2)}, u32[]{:S(2)}) collective-permute-start(bf16[2,16,40,128]{3,2,1,0:T(8,128)(2,1)S(1)} %bitcast.8), channel_id=1, source_target_pairs={{0,4},{4,0},{1,5},{5,1},{2,6},{6,2},{3,7},{7,3},{8,12},{12,8},{9,1... | collective-permute-start | bytes 983048 | tf_op jit(solution)/shard_map/ppermute | solution.py:319
  28.8 1.3 %collective-permute-done = bf16[2,16,40,128]{3,2,1,0:T(8,128)(2,1)S(1)} collective-permute-done((bf16[2,16,40,128]{3,2,1,0:T(8,128)(2,1)S(1)}, bf16[2,16,40,128]{3,2,1,0:T(8,128)(2,1)S(1)}, u32[]{:S(2)}, u32[]{:S(2)}) %collective-permute-start) | collective-permute-done | bytes 327712 | tf_op jit(solution)/shard_map/ppermute | solution.py:319
  30.1 19.3 %all_to_all.10.in_ref = bf16[16,40,128]{2,1,0:T(8,128)(2,1)S(1)} all-to-all(bf16[16,40,128]{2,1,0:T(8,128)(2,1)S(1)} %fusion), channel_id=1, replica_groups=mesh['zh'=4,'zl'=2,'x'=4,'core'=2,'scene'=4] {'zh','scene'}, dimensions={0} | all-to-all | bytes 327680 | tf_op jit(solution)/shard_map/all_to_all | solution.py:323
  49.4 0.8 %merge_parts.1 = bf16[64,320]{1,0:T(8,128)(2,1)} custom-call(bf16[16,40,128]{2,1,0:T(8,128)(2,1)S(1)} %all_to_all.10.in_ref), custom_call_target="tpu_custom_call" | custom-call | tf_op jit(solution)/shard_map/merge_parts/pallas_call | solution.py:304
  (1 shorter events, 0.0 us)
Async XLA Ops:
  5.1 16.5 %all-to-all-start = ((bf16[8,176,256]{2,1,0:T(8,128)(2,1)}), bf16[8,176,256]{2,1,0:T(8,128)(2,1)S(1)}, u32[]{:S(2)}, u32[]{:S(2)}) async-start(bf16[8,176,256]{2,1,0:T(8,128)(2,1)} %send_slots.2), calls=%async_computation | async-start | bytes 1441792 | tf_op jit(solution)/shard_map/all_to_all | solution.py:316
  26.7 3.3 %collective-permute-start = (bf16[2,16,40,128]{3,2,1,0:T(8,128)(2,1)S(1)}, bf16[2,16,40,128]{3,2,1,0:T(8,128)(2,1)S(1)}, u32[]{:S(2)}, u32[]{:S(2)}) collective-permute-start(bf16[2,16,40,128]{3,2,1,0:T(8,128)(2,1)S(1)} %bitcast.8), channel_id=1, source_target_pairs={{0,4},{4,0},{1,5},{5,1},{2,6},{6,2},{3,7},{7,3},{8,12},{12,8},{9,1... | collective-permute-start | bytes 983048 | tf_op jit(solution)/shard_map/ppermute | solution.py:319

commit v6 on v4

--- a/solution.py
+++ b/solution.py
@@ -121,7 +121,11 @@
         out_ref[dest, SLOT_ROWS:ROWS, :] = context
 
 
-def pool_kernel(in_ref, out_ref, slots_ref, acc_ref, val_ref, word_ref):
+def own_core():
+    return lax.axis_index("core")
+
+
+def pool_kernel(in_ref, mine_ref, away_ref, slots_ref, acc_ref, val_ref, word_ref):
     for src in range(GROUP):
         slots_ref[src * SLOT_ROWS : (src + 1) * SLOT_ROWS, :] = in_ref[src, :SLOT_ROWS, :].astype(F32)
     acc_ref[...] = jnp.zeros(acc_ref.shape, F32)
@@ -191,12 +195,14 @@
         gather(lax.rem(batches - 1, 2), b, items[b])
 
     left = lax.broadcasted_iota(jnp.int32, (C // 2, 128), 1) < 64
-    for z in range(ZS):
-        for t in range(2):
-            a = acc_ref[z, : C // 2, t * 128 : (t + 1) * 128]
-            b = acc_ref[z, C // 2 :, t * 128 : (t + 1) * 128]
-            out_ref[z * 4 + 2 * t] = jnp.where(left, a, pltpu.roll(b, 64, 1)).astype(BF)
-            out_ref[z * 4 + 2 * t + 1] = jnp.where(left, pltpu.roll(a, 64, 1), b).astype(BF)
+    core = own_core()
+    for part, ref in ((core, mine_ref), (1 - core, away_ref)):
+        for z in range(ZS // 2):
+            for t in range(2):
+                a = acc_ref[part * (ZS // 2) + z, : C // 2, t * 128 : (t + 1) * 128]
+                b = acc_ref[part * (ZS // 2) + z, C // 2 :, t * 128 : (t + 1) * 128]
+                ref[z * 4 + 2 * t] = jnp.where(left, a, pltpu.roll(b, 64, 1)).astype(ref.dtype)
+                ref[z * 4 + 2 * t + 1] = jnp.where(left, pltpu.roll(a, 64, 1), b).astype(ref.dtype)
 
 
 def merge_kernel(in_ref, out_ref):
@@ -244,9 +250,12 @@
 def pool(slots):
     return pl.pallas_call(
         pool_kernel,
-        out_shape=jax.ShapeDtypeStruct((ZS * 4, C // 2, 128), BF),
+        out_shape=[
+            jax.ShapeDtypeStruct((2 * ZS, C // 2, 128), F32),
+            jax.ShapeDtypeStruct((2 * ZS, C // 2, 128), BF),
+        ],
         in_specs=[VMEM],
-        out_specs=VMEM,
+        out_specs=[VMEM, VMEM],
         scratch_shapes=[
             pltpu.VMEM((GROUP * SLOT_ROWS, CHUNK), F32),
             pltpu.VMEM((ZS + 1, C, CELLS), F32),
@@ -272,11 +281,9 @@
 def body(context, depth_logits, send_count, slot_point, slot_cell):
     slots = send(send_count[0, 0], depth_logits[0], context[0], slot_point[0, 0], slot_cell[0, 0])
     slots = lax.all_to_all(slots, ("zl", "x"), 0, 0, tiled=True)
-    mine = pool(slots).reshape(2, 2 * ZS, C // 2, 128)
-    theirs = lax.ppermute(mine, "core", [(0, 1), (1, 0)])
-    core = lax.axis_index("core")
-    half = [lax.dynamic_index_in_dim(v, core, 0, keepdims=False).astype(F32) for v in (mine, theirs)]
-    partials = (half[0] + half[1]).astype(BF)
+    mine, away = pool(slots)
+    theirs = lax.ppermute(away, "core", [(0, 1), (1, 0)])
+    partials = (mine + theirs.astype(F32)).astype(BF)
     partials = lax.all_to_all(partials, ("zh", "scene"), 0, 0, tiled=True)
     return merge(partials)
 

time: 51.2 us -> 51 us (level)
  no operation moved by 1% of the time
where the time goes in v6:
time: 51 us; the launch traced here: 50.8 us
  blocking collectives  36.3 us (71%)
  Pallas kernels  11 us (22%)
  starting transfers between devices  2.42 us (5%)
  waiting for transfers between devices  1.03 us (2%)
    all_to_all x1, blocking collectives, body(): partials = lax.all_to_all(partials, ('zh', 'scene'), 0, 0, tiled=True)  19.4 us
    all_to_all x1, blocking collectives, body(): slots = lax.all_to_all(slots, ('zl', 'x'), 0, 0, tiled=True)  16.9 us
    pallas_call x1, Pallas kernels, pool(): pl.pallas_call(pool_kernel, out_shape=[jax.ShapeDtypeStruct((2 * ZS, C //...  5.68 us
    pallas_call x1, Pallas kernels, send(): pl.pallas_call(send_kernel, out_shape=pltpu.VMEM((GROUP, ROWS, PIX), BF),...  4.57 us
    ppermute x1, starting transfers between devices, body(): theirs = lax.ppermute(away, 'core', [(0, 1), (1, 0)])  2.42 us
    ppermute x1, waiting for transfers between devices, body(): theirs = lax.ppermute(away, 'core', [(0, 1), (1, 0)])  1.03 us
  transfers between devices with their start and end apart: 1, of which 1 were waited for; matrix products, arithmetic and copies ran while one was open for 0% of the time, Pallas kernels for 0%

profile of v6, /device:TPU:1, one launch (start us, length us, event | category | flops | bytes accessed | tf_op | source)
XLA Modules:
  0.0 50.8 jit_solution(5482903360048992985)
XLA Ops:
  0.0 4.6 %send_slots.1 = bf16[8,176,256]{2,1,0:T(8,128)(2,1)S(1)} custom-call(s32[64]{0:T(128)} %bitcast.9, f32[112,256]{1,0:T(8,128)} %bitcast.7, bf16[80,256]{1,0:T(8,128)(2,1)} %bitcast.8, s32[64,1024]{1,0:T(8,128)} %bitcast.5, s32[64,1024]{1,0:T(8,128)} %bitcast.6), custom_call_target="tpu_custom_call" | custom-call | tf_op jit(solution)/shard_map/send_slots/pallas_call | solution.py:226
  4.6 16.9 %all_to_all.10.in_ref = bf16[8,176,256]{2,1,0:T(8,128)(2,1)S(1)} all-to-all(bf16[8,176,256]{2,1,0:T(8,128)(2,1)S(1)} %send_slots.1), channel_id=1, replica_groups=mesh['zh'=4,'zl'=2,'x'=4,'core'=2,'scene'=4] {'zl','x'}, dimensions={0} | all-to-all | bytes 1441792 | tf_op jit(solution)/shard_map/all_to_all | solution.py:283
  21.5 5.7 %pool_slots.1 = (f32[16,40,128]{2,1,0:T(8,128)S(1)}, bf16[16,40,128]{2,1,0:T(8,128)(2,1)S(1)}) custom-call(bf16[8,176,256]{2,1,0:T(8,128)(2,1)S(1)} %all_to_all.10.in_ref), custom_call_target="tpu_custom_call" | custom-call | tf_op jit(solution)/shard_map/pool_slots/pallas_call | solution.py:251
  27.1 2.4 %collective-permute-start = (bf16[16,40,128]{2,1,0:T(8,128)(2,1)S(1)}, bf16[16,40,128]{2,1,0:T(8,128)(2,1)S(1)}, u32[]{:S(2)}, u32[]{:S(2)}) collective-permute-start(bf16[16,40,128]{2,1,0:T(8,128)(2,1)S(1)} %get-tuple-element.8), channel_id=1, source_target_pairs={{0,4},{4,0},{1,5},{5,1},{2,6},{6,2},{3,7},{7,3},{8,12},{12,8},{9,1... | collective-permute-start | bytes 491528 | tf_op jit(solution)/shard_map/ppermute | solution.py:285
  29.6 1.0 %collective-permute-done = bf16[16,40,128]{2,1,0:T(8,128)(2,1)S(1)} collective-permute-done((bf16[16,40,128]{2,1,0:T(8,128)(2,1)S(1)}, bf16[16,40,128]{2,1,0:T(8,128)(2,1)S(1)}, u32[]{:S(2)}, u32[]{:S(2)}) %collective-permute-start) | collective-permute-done | bytes 163872 | tf_op jit(solution)/shard_map/ppermute | solution.py:285
  30.6 19.4 %all_to_all.11.in_ref = bf16[16,40,128]{2,1,0:T(8,128)(2,1)S(1)} all-to-all(bf16[16,40,128]{2,1,0:T(8,128)(2,1)S(1)} %add_convert_fusion), channel_id=1, replica_groups=mesh['zh'=4,'zl'=2,'x'=4,'core'=2,'scene'=4] {'zh','scene'}, dimensions={0} | all-to-all | bytes 327680 | tf_op jit(solution)/shard_map/all_to_all | solution.py:287
  50.0 0.8 %merge_parts.1 = bf16[64,320]{1,0:T(8,128)(2,1)} custom-call(bf16[16,40,128]{2,1,0:T(8,128)(2,1)S(1)} %all_to_all.11.in_ref), custom_call_target="tpu_custom_call" | custom-call | tf_op jit(solution)/shard_map/merge_parts/pallas_call | solution.py:271
  (1 shorter events, 0.0 us)
Async XLA Ops:
  27.1 3.4 %collective-permute-start = (bf16[16,40,128]{2,1,0:T(8,128)(2,1)S(1)}, bf16[16,40,128]{2,1,0:T(8,128)(2,1)S(1)}, u32[]{:S(2)}, u32[]{:S(2)}) collective-permute-start(bf16[16,40,128]{2,1,0:T(8,128)(2,1)S(1)} %get-tuple-element.8), channel_id=1, source_target_pairs={{0,4},{4,0},{1,5},{5,1},{2,6},{6,2},{3,7},{7,3},{8,12},{12,8},{9,1... | collective-permute-start | bytes 491528 | tf_op jit(solution)/shard_map/ppermute | solution.py:285

commit v7 on v6

--- a/solution.py
+++ b/solution.py
@@ -133,7 +133,7 @@
     rows = ZS * NCH
     lane0 = lax.broadcasted_iota(jnp.int32, (ZS, 128), 1) == 0
     digit = jnp.left_shift(1, 3 * lax.broadcasted_iota(jnp.int32, (ZS, 128), 0)).astype(F32)
-    total = jnp.int32(0)
+    everywhere = jnp.zeros((ZS, 128), F32)
     for src in range(GROUP):
         live = jnp.zeros((ZS, 128), F32)
         for j in range(NCH):
@@ -143,7 +143,8 @@
                 on = on | True
             live = live + jnp.where(lane0 & on, 1.0, 0.0)
         word_ref[src] = jnp.sum(live * digit).astype(jnp.int32)
-        total = total + jnp.sum(live).astype(jnp.int32)
+        everywhere = everywhere + live
+    total = jnp.sum(everywhere).astype(jnp.int32)
     word_ref[GROUP] = 0
 
     def select(slot, b, state):

time: 51 us -> 51 us (level)
  no operation moved by 1% of the time
where the time goes in v7:
time: 51 us; the launch traced here: 50.9 us
  blocking collectives  36.3 us (71%)
  Pallas kernels  11.1 us (22%)
  starting transfers between devices  2.42 us (5%)
  waiting for transfers between devices  1.03 us (2%)
    all_to_all x1, blocking collectives, body(): partials = lax.all_to_all(partials, ('zh', 'scene'), 0, 0, tiled=True)  19.4 us
    all_to_all x1, blocking collectives, body(): slots = lax.all_to_all(slots, ('zl', 'x'), 0, 0, tiled=True)  16.9 us
    pallas_call x1, Pallas kernels, pool(): pl.pallas_call(pool_kernel, out_shape=[jax.ShapeDtypeStruct((2 * ZS, C //...  5.71 us
    pallas_call x1, Pallas kernels, send(): pl.pallas_call(send_kernel, out_shape=pltpu.VMEM((GROUP, ROWS, PIX), BF),...  4.59 us
    ppermute x1, starting transfers between devices, body(): theirs = lax.ppermute(away, 'core', [(0, 1), (1, 0)])  2.42 us
    ppermute x1, waiting for transfers between devices, body(): theirs = lax.ppermute(away, 'core', [(0, 1), (1, 0)])  1.03 us
  transfers between devices with their start and end apart: 1, of which 1 were waited for; matrix products, arithmetic and copies ran while one was open for 0% of the time, Pallas kernels for 0%

profile of v7, /device:TPU:1, one launch (start us, length us, event | category | flops | bytes accessed | tf_op | source)
XLA Modules:
  0.0 50.9 jit_solution(12819947342277000685)
XLA Ops:
  0.0 4.6 %send_slots.1 = bf16[8,176,256]{2,1,0:T(8,128)(2,1)S(1)} custom-call(s32[64]{0:T(128)} %bitcast.9, f32[112,256]{1,0:T(8,128)} %bitcast.7, bf16[80,256]{1,0:T(8,128)(2,1)} %bitcast.8, s32[64,1024]{1,0:T(8,128)} %bitcast.5, s32[64,1024]{1,0:T(8,128)} %bitcast.6), custom_call_target="tpu_custom_call" | custom-call | tf_op jit(solution)/shard_map/send_slots/pallas_call | solution.py:227
  4.6 16.9 %all_to_all.10.in_ref = bf16[8,176,256]{2,1,0:T(8,128)(2,1)S(1)} all-to-all(bf16[8,176,256]{2,1,0:T(8,128)(2,1)S(1)} %send_slots.1), channel_id=1, replica_groups=mesh['zh'=4,'zl'=2,'x'=4,'core'=2,'scene'=4] {'zl','x'}, dimensions={0} | all-to-all | bytes 1441792 | tf_op jit(solution)/shard_map/all_to_all | solution.py:284
  21.5 5.7 %pool_slots.1 = (f32[16,40,128]{2,1,0:T(8,128)S(1)}, bf16[16,40,128]{2,1,0:T(8,128)(2,1)S(1)}) custom-call(bf16[8,176,256]{2,1,0:T(8,128)(2,1)S(1)} %all_to_all.10.in_ref), custom_call_target="tpu_custom_call" | custom-call | tf_op jit(solution)/shard_map/pool_slots/pallas_call | solution.py:252
  27.2 2.4 %collective-permute-start = (bf16[16,40,128]{2,1,0:T(8,128)(2,1)S(1)}, bf16[16,40,128]{2,1,0:T(8,128)(2,1)S(1)}, u32[]{:S(2)}, u32[]{:S(2)}) collective-permute-start(bf16[16,40,128]{2,1,0:T(8,128)(2,1)S(1)} %get-tuple-element.8), channel_id=1, source_target_pairs={{0,4},{4,0},{1,5},{5,1},{2,6},{6,2},{3,7},{7,3},{8,12},{12,8},{9,1... | collective-permute-start | bytes 491528 | tf_op jit(solution)/shard_map/ppermute | solution.py:286
  29.6 1.0 %collective-permute-done = bf16[16,40,128]{2,1,0:T(8,128)(2,1)S(1)} collective-permute-done((bf16[16,40,128]{2,1,0:T(8,128)(2,1)S(1)}, bf16[16,40,128]{2,1,0:T(8,128)(2,1)S(1)}, u32[]{:S(2)}, u32[]{:S(2)}) %collective-permute-start) | collective-permute-done | bytes 163872 | tf_op jit(solution)/shard_map/ppermute | solution.py:286
  30.7 19.4 %all_to_all.11.in_ref = bf16[16,40,128]{2,1,0:T(8,128)(2,1)S(1)} all-to-all(bf16[16,40,128]{2,1,0:T(8,128)(2,1)S(1)} %add_convert_fusion), channel_id=1, replica_groups=mesh['zh'=4,'zl'=2,'x'=4,'core'=2,'scene'=4] {'zh','scene'}, dimensions={0} | all-to-all | bytes 327680 | tf_op jit(solution)/shard_map/all_to_all | solution.py:288
  50.1 0.8 %merge_parts.1 = bf16[64,320]{1,0:T(8,128)(2,1)} custom-call(bf16[16,40,128]{2,1,0:T(8,128)(2,1)S(1)} %all_to_all.11.in_ref), custom_call_target="tpu_custom_call" | custom-call | tf_op jit(solution)/shard_map/merge_parts/pallas_call | solution.py:272
  (1 shorter events, 0.0 us)
Async XLA Ops:
  27.2 3.4 %collective-permute-start = (bf16[16,40,128]{2,1,0:T(8,128)(2,1)S(1)}, bf16[16,40,128]{2,1,0:T(8,128)(2,1)S(1)}, u32[]{:S(2)}, u32[]{:S(2)}) collective-permute-start(bf16[16,40,128]{2,1,0:T(8,128)(2,1)S(1)} %get-tuple-element.8), channel_id=1, source_target_pairs={{0,4},{4,0},{1,5},{5,1},{2,6},{6,2},{3,7},{7,3},{8,12},{12,8},{9,1... | collective-permute-start | bytes 491528 | tf_op jit(solution)/shard_map/ppermute | solution.py:286
